TPU v7x, 256 devices: a whole 4x4x8 slice. The times are simulated.
256 devices in a mesh: dp: 128 (over z, y, x), mp: 2 (over core).
Axes of the slice: x: 4, y: 4, z: 8, core: 2. Of those that a mesh axis runs over, the one named last changes fastest.
Arguments:
- points: bfloat16 [131072, 1024], P(('dp', 'mp')), may hold values from -6 to 6
- centroids: bfloat16 [4096, 1024], P('mp'), may hold values from -6 to 6
- assign: int32 [131072], P(('dp', 'mp')), may hold values from 0 to 4095
- keep_mask: int32 [131072], P(('dp', 'mp')), may hold values 0 or 1
Outputs:
- new_centroids: float32 [4096, 1024], P('mp')
- row_cost: float32 [131072], P(('dp', 'mp'))
All inputs are finite; a program needn't handle non-finite values. No bound on the sum of `keep_mask` on one device may be relied on, other than what follows from the above.
Results may differ from a plain program's by a relative error of at most 0.0008.
Values may be sent and summed in bfloat16 or wider, within the bound.
A program may use at most 128 MiB of HBM per device.

v0:
```python
import functools

import jax
import jax.numpy as jnp
from jax import lax
from jax.experimental import pallas as pl
from jax.experimental.pallas import tpu as pltpu
from jax.sharding import Mesh
from jax.sharding import PartitionSpec as P

STEPS = 32000.0
TINY = 2.0**-100
EXTRA = 8
PLANE = 4
LANES = 128


def remote(src, dst, send, recv, device):
    return pltpu.make_async_remote_copy(
        src_ref=src,
        dst_ref=dst,
        send_sem=send,
        recv_sem=recv,
        device_id=device,
        device_id_type=pl.DeviceIdType.MESH,
    )


def greet(peers):
    barrier = pltpu.get_barrier_semaphore()
    for peer in peers:
        pl.semaphore_signal(barrier, inc=1, device_id=peer, device_id_type=pl.DeviceIdType.MESH)
    pl.semaphore_wait(barrier, len(peers))


def update_kernel(
    z_n, shard_rows, p_ref, id_ref, prior_ref, out_ref,
    near, idn, acc, mrecv, red, zrecv,
    ps, pr, ids_s, ids_r, ms, mr, zs, zr, gs, gr, xs, xr, ys, yr, ds_, dr,
):
    z, q, m = lax.axis_index("z"), lax.axis_index("q"), lax.axis_index("mp")
    nx = q + 1 - 2 * lax.rem(q, 2)
    ny = lax.rem(q + 2, PLANE)
    nd = ny + 1 - 2 * lax.rem(ny, 2)
    other = 1 - m
    rows, width = p_ref.shape
    block = prior_ref.shape[0]
    half = rows // 2
    peers = [(z, nx, m), (z, ny, m), (z, nd, m), (z, q, other)]
    greet(peers + [(lax.rem(z + d, z_n), q, m) for d in range(1, z_n)])

    id_copies = [
        remote(id_ref, idn.at[k], ids_s.at[k], ids_r.at[k], (z, to, m))
        for k, to in enumerate((nx, ny, nd))
    ]
    for c in id_copies:
        c.start()
    lo, hi = pl.ds(0, half), pl.ds(half, half)

    def piece(k, src, slot, part, to):
        return remote(src, near.at[slot, part], ps.at[k], pr.at[k], (z, to, m))

    a = piece(0, p_ref.at[lo], 0, lo, nx)
    c = piece(1, p_ref.at[hi], 1, hi, ny)
    b = piece(2, p_ref.at[hi], 0, hi, nx)
    d_ = piece(3, p_ref.at[lo], 1, lo, ny)
    e = piece(4, near.at[0, lo], 2, lo, ny)
    f = piece(5, near.at[1, hi], 2, hi, nx)
    for copy in (a, c, b, d_):
        copy.start()

    def add(ids, pts, first):
        def tile(t, carry):
            base = (t // z_n) * shard_rows + (lax.rem(t, z_n) * PLANE + q) * block
            row = base + lax.broadcasted_iota(jnp.int32, (block, rows), 0)
            hit = jnp.where(row == ids[0:1, :], 1.0, 0.0)
            part = jnp.dot(hit.astype(jnp.bfloat16), pts[...], preferred_element_type=jnp.float32)
            count = jnp.broadcast_to(jnp.sum(hit, axis=1, keepdims=True), (block, LANES))
            if first:
                acc[t, :, :width] = part
                acc[t, :, width:] = count
            else:
                acc[t, :, :width] += part
                acc[t, :, width:] += count
            return carry

        lax.fori_loop(0, 2 * z_n, tile, 0)

    add(id_ref, p_ref, True)
    a.wait_recv()
    e.start()
    c.wait_recv()
    f.start()
    for copy in id_copies:
        copy.wait_recv()
    b.wait_recv()
    add(idn.at[0], near.at[0], False)
    d_.wait_recv()
    add(idn.at[1], near.at[1], False)
    e.wait_recv()
    f.wait_recv()
    add(idn.at[2], near.at[2], False)

    mcopy = remote(acc.at[pl.ds(other * z_n, z_n)], mrecv, ms, mr, (z, q, other))
    mcopy.start()
    mcopy.wait_recv()

    zcopies = []
    for k in range(1, z_n + 1):
        to = lax.rem(z + k, z_n)
        red[to] = acc[m * z_n + to] + mrecv[to]
        if k < z_n:
            copy = remote(red.at[to], zrecv.at[k - 1], zs.at[k - 1], zr.at[k - 1], (to, q, m))
            copy.start()
            zcopies.append(copy)
    for k in range(1, z_n):
        zcopies[k - 1].wait_recv()
        red[z] += zrecv[k - 1]

    sums = red[z, :, :width]
    count = red[z, :, width : width + 1]
    fresh = jnp.where(
        count > 0.5, sums / jnp.maximum(count, 1.0), prior_ref[...].astype(jnp.float32)
    )
    own = z * PLANE + q
    half_w = width // 2
    top = jnp.max(jnp.abs(fresh), axis=1, keepdims=True)
    power = jnp.ceil(jnp.log2(jnp.maximum(top, TINY)))
    code = jnp.floor(fresh * jnp.exp2(-power) * STEPS + 0.5).astype(jnp.int32)
    out_ref[own, :block] = (code[:, :half_w] << 16) | (code[:, half_w:] & 0xFFFF)
    at_row = lax.broadcasted_iota(jnp.int32, (block, LANES), 0)
    at_lane = lax.broadcasted_iota(jnp.int32, (block, LANES), 1)
    flat = jnp.sum(jnp.where(at_row == at_lane, power, 0.0), axis=0, keepdims=True)
    out_ref[own, block:] = jnp.zeros((EXTRA, half_w), jnp.int32)
    out_ref[own, block:, :LANES] = jnp.broadcast_to(flat.astype(jnp.int32), (EXTRA, LANES))

    def pass_on(index, send, recv, device):
        copy = remote(out_ref.at[index], out_ref.at[index], send, recv, device)
        copy.start()
        return copy

    gcopies = [
        pass_on(own, gs.at[k - 1], gr.at[k - 1], (lax.rem(z + k, z_n), q, m))
        for k in range(1, z_n)
    ]
    xc, yc, dc = [], [], []

    def relay(k):
        base = lax.rem(z + z_n - k, z_n) * PLANE
        if k % 2 == 0:
            xc[k].wait_recv()
            dc.append(pass_on(base + nx, ds_.at[k], dr.at[k], (z, ny, m)))
        else:
            yc[k].wait_recv()
            dc.append(pass_on(base + ny, ds_.at[k], dr.at[k], (z, nx, m)))

    for k in range(z_n):
        mine = lax.rem(z + z_n - k, z_n) * PLANE + q
        if k > 0:
            gcopies[k - 1].wait_recv()
        xc.append(pass_on(mine, xs.at[k], xr.at[k], (z, nx, m)))
        yc.append(pass_on(mine, ys.at[k], yr.at[k], (z, ny, m)))
        if k > 0:
            relay(k - 1)
    relay(z_n - 1)
    for k in range(z_n):
        if k % 2 == 0:
            yc[k].wait_recv()
        else:
            xc[k].wait_recv()
        dc[k].wait_recv()
    for copy in id_copies + [a, b, c, d_, e, f, mcopy] + zcopies + gcopies + xc + yc + dc:
        copy.wait_send()


def shards(points, centroids, assign, keep_mask):
    rows, width = points.shape
    shard_rows = centroids.shape[0]
    z_n = lax.axis_size("z")
    dp_n = z_n * PLANE
    block = shard_rows // dp_n
    own = lax.axis_index("z") * PLANE + lax.axis_index("q")
    ids = jnp.where(keep_mask > 0, assign, -1)
    ids = jnp.broadcast_to(ids[None, :], (8, rows))
    prior = lax.dynamic_slice_in_dim(centroids, own * block, block, 0)
    vmem = pl.BlockSpec(memory_space=pltpu.VMEM)
    dma = pltpu.SemaphoreType.DMA
    wide = width + LANES
    back = pl.pallas_call(
        functools.partial(update_kernel, z_n, shard_rows),
        out_shape=jax.ShapeDtypeStruct((dp_n, block + EXTRA, width // 2), jnp.int32),
        in_specs=[vmem] * 3,
        out_specs=vmem,
        scratch_shapes=[
            pltpu.VMEM((3, rows, width), points.dtype),
            pltpu.VMEM((3, 8, rows), jnp.int32),
            pltpu.VMEM((2 * z_n, block, wide), jnp.float32),
            pltpu.VMEM((z_n, block, wide), jnp.float32),
            pltpu.VMEM((z_n, block, wide), jnp.float32),
            pltpu.VMEM((z_n - 1, block, wide), jnp.float32),
            dma((6,)), dma((6,)), dma((3,)), dma((3,)), dma, dma,
            dma((z_n - 1,)), dma((z_n - 1,)), dma((z_n - 1,)), dma((z_n - 1,)),
            dma((z_n,)), dma((z_n,)), dma((z_n,)), dma((z_n,)), dma((z_n,)), dma((z_n,)),
        ],
        compiler_params=pltpu.CompilerParams(
            collective_id=0, has_side_effects=True, vmem_limit_bytes=48 * 1024 * 1024
        ),
        cost_estimate=pl.CostEstimate(
            flops=0, bytes_accessed=200 * 1024 * 1024, transcendentals=0
        ),
    )(points, ids, prior)
    codes = back[:, :block]
    powers = back[:, block, :block].astype(jnp.float32)
    scale = (jnp.exp2(powers) / STEPS)[:, :, None]
    pair = jnp.concatenate([codes >> 16, (codes << 16) >> 16], axis=2)
    new_centroids = (pair.astype(jnp.float32) * scale).reshape(shard_rows, width)

    piece = lax.all_gather(centroids, "mp", axis=0, tiled=True)
    inner = lax.dot_general(
        points, piece, (((1,), (1,)), ((), ())), preferred_element_type=jnp.float32
    )
    point_f = points.astype(jnp.float32)
    point_sq = jnp.sum(point_f * point_f, axis=1)
    piece_f = piece.astype(jnp.float32)
    cent_sq = jnp.sum(piece_f * piece_f, axis=1)
    dist = point_sq[:, None] - 2.0 * inner + cent_sq[None, :]
    row_cost = jnp.min(dist, axis=1) / width
    return new_centroids, row_cost


def solution(mesh):
    dp, mp = mesh.shape["dp"], mesh.shape["mp"]
    grid = Mesh(mesh.devices.reshape(dp // PLANE, PLANE, mp), ("z", "q", "mp"))
    rows = ("z", "q", "mp")
    in_specs = (P(rows, None), P("mp", None), P(rows), P(rows))
    out_specs = (P("mp", None), P(rows))
    return jax.shard_map(shards, mesh=grid, in_specs=in_specs, out_specs=out_specs, check_vma=False)
```

profile of v0, /device:TPU:2, one launch (start us, length us, event | category | flops | bytes accessed | tf_op | source)
XLA Modules:
  0.0 310.2 jit_solution(801685955092993909)
XLA Ops:
  7.2 0.0 copy-start.1
  7.2 0.0 all-gather.2.cloned.1.call-start
  7.2 0.7 all-gather.2.cloned.1.call-update
  7.9 0.8 constant_dynamic-slice_fusion.prior_ref
  8.7 0.7 compare_select_fusion
  9.4 0.0 copy-start
  9.4 1.2 copy-done
  10.6 272.6 %shard_map.59 = s32[128,24,512]{2,1,0:T(8,128)} custom-call(bf16[512,1024]{1,0:T(8,128)(2,1)S(1)} %copy-done, s32[8,512]{1,0:T(8,128)S(1)} %broadcast_in_dim.7.id_ref, bf16[16,1024]{1,0:T(8,128)(2,1)S(1)} %constant_dynamic-slice_fusion.prior_ref), custom_call_target="tpu_custom_call" | custom-call | bytes 209715200 | tf_op jit(solution)/shard_map/pallas_call | solution.py:189
  283.3 1.3 multiply_reduce_fusion.2
  284.6 0.1 div.16
  284.6 0.0 copy-done.1
  284.6 0.3 multiply_reduce_fusion.1
  284.9 3.3 %slice_shift-right-arithmetic_fusion = (s32[128,16,512]{2,1,0:T(8,128)S(1)}, s32[128,16,512]{2,1,0:T(8,128)S(1)}) fusion(s32[128,24,512]{2,1,0:T(8,128)} %shard_map.59), kind=kLoop, calls=%fused_computation.5 | loop fusion | flops 3145728 | bytes 12582912 | tf_op jit(solution)/shard_map/shift_right_arithmetic | solution.py:215
  288.2 3.8 %fusion = f32[2048,1024]{1,0:T(8,128)} fusion(s32[2048,512]{1,0:T(8,128)S(1)} %bitcast.5, s32[2048,512]{1,0:T(8,128)S(1)} %bitcast.4, f32[2048]{0:T(1024)S(1)} %div.16), kind=kLoop, calls=%fused_computation.2 | loop fusion | flops 6291456 | bytes 16785408 | tf_op jit(solution)/shard_map/mul | solution.py:216
  292.0 0.0 all-gather.2.cloned.1.call-done
  292.0 0.0 copy-start.2
  292.0 5.2 %multiply_reduce_fusion = f32[4096]{0:T(1024)S(1)} fusion(bf16[4096,1024]{1,0:T(8,128)(2,1)} %all-gather.2.cloned.1.call-done), kind=kLoop, calls=%fused_computation | loop fusion | flops 12578816 | bytes 8404992 | tf_op jit(solution)/shard_map/reduce_sum | solution.py:225
  297.2 0.5 copy-done.2
  297.7 5.1 %add_reduce_fusion = f32[512]{0:T(512)S(1)} fusion(bf16[512,1024]{1,0:T(8,128)(2,1)S(1)} %copy-done.1, bf16[4096,1024]{1,0:T(8,128)(2,1)S(1)} %copy-done.2, f32[4096]{0:T(1024)S(1)} %multiply_reduce_fusion, f32[512]{0:T(512)S(1)} %multiply_reduce_fusion.1), kind=kOutput, calls=%fused_computation.3 | convolution fusion | flops 4303355392 | bytes 9457664 | tf_op jit(solution)/shard_map/dot_general | solution.py:219
  302.8 0.6 broadcast_multiply_fusion
  (1 shorter events, 0.0 us)
Async XLA Ops:
  7.2 277.5 %copy-start.1 = (bf16[512,1024]{1,0:T(8,128)(2,1)S(1)}, bf16[512,1024]{1,0:T(8,128)(2,1)}, u32[]{:S(2)}) copy-start(bf16[512,1024]{1,0:T(8,128)(2,1)} %p_ref.1) | copy-start | bytes 3145732
  7.2 284.8 %all-gather.2.cloned.1.call-start = ((), (), s32[]{:S(2)}) async-start(), calls=%async_computation | async-start | bytes 12582912 | tf_op jit(solution)/shard_map/all_gather | solution.py:218
  9.4 1.2 copy-start
  292.0 5.8 %copy-start.2 = (bf16[4096,1024]{1,0:T(8,128)(2,1)S(1)}, bf16[4096,1024]{1,0:T(8,128)(2,1)}, u32[]{:S(2)}) copy-start(bf16[4096,1024]{1,0:T(8,128)(2,1)} %all-gather.2.cloned.1.call-done) | copy-start | bytes 25165828
Sparse Core Ops, SparseCore 0:
  9.8 28.1 all-gather.1
where the time goes:
time: 314 us; the launch traced here: 310 us
  Pallas kernels  273 us (87%)
  other arithmetic  15.1 us (5%)
  between operations  14.1 us (4%)
  matrix products  5.07 us (2%)
    pallas_call x1, Pallas kernels, shards(): pl.pallas_call(functools.partial(update_kernel, z_n, shard_rows), out_sha...  273 us
  transfers between devices with their start and end apart: 1, of which 0 were waited for; matrix products, arithmetic and copies ran while one was open for 3% of the time, Pallas kernels for 88%

commit v1 on v0

v1 whole, which is shorter than its diff:
```python
import jax
import jax.numpy as jnp
from jax import lax
from jax.experimental import pallas as pl
from jax.experimental.pallas import tpu as pltpu
from jax.sharding import Mesh
from jax.sharding import PartitionSpec as P

STEPS = 32000.0
TINY = 2.0**-100
NX, NY, NZ = 4, 4, 8
LANES = 128
FEATS = 256
CROWS = 512
OWN = 64
TILE = 256
MESH_ID = pl.DeviceIdType.MESH


def encode(v):
    top = jnp.maximum(jnp.max(jnp.abs(v), axis=1, keepdims=True), TINY)
    code = jnp.floor(v * (STEPS / top) + 0.5).astype(jnp.int32)
    return (code[:, :LANES] << 16) | (code[:, LANES:] & 0xFFFF), top * (1.0 / STEPS)


def decode(words, step):
    high = (words >> 16).astype(jnp.float32)
    low = ((words << 16) >> 16).astype(jnp.float32)
    return high * step, low * step


def lane_eye(rows, shift=0):
    at_row = lax.broadcasted_iota(jnp.int32, (rows, LANES), 0)
    at_lane = lax.broadcasted_iota(jnp.int32, (rows, LANES), 1)
    return at_lane == at_row + shift


def to_row(col, eye):
    return jnp.sum(jnp.where(eye, col, 0.0), axis=0, keepdims=True)


def to_col(row, eye):
    return jnp.sum(jnp.where(eye, row, 0.0), axis=1, keepdims=True)


def update_kernel(
    p_hbm, c_hbm, assign_ref, keep_ref, words_ref, steps_ref, cost_ref,
    pv, cv, near, ids, relay, best, acc, cnt,
    ysend, yaux, yrecv, yauxr, zsend, zaux, zrecv, zauxr,
    send_sem, recv_sem, local_sem,
):
    z, y, x, m = (lax.axis_index(n) for n in ("z", "y", "x", "mp"))
    xr, xl, xo = (lax.rem(x + d, NX) for d in (1, 3, 2))
    yr, yl, yo = (lax.rem(y + d, NY) for d in (1, 3, 2))
    zat = lambda d: lax.rem(z + d + NZ, NZ)
    other = 1 - m
    used = []

    def remote(src, dst, device):
        k = len(used)
        copy = pltpu.make_async_remote_copy(
            src_ref=src, dst_ref=dst, send_sem=send_sem.at[k], recv_sem=recv_sem.at[k],
            device_id=device, device_id_type=MESH_ID,
        )
        copy.start()
        used.append(copy)
        return copy

    at_x = lambda to: (z, y, to, m)
    at_y = lambda to: (z, to, x, m)
    at_z = lambda to: (to, y, x, m)
    partner = (z, y, x, other)

    load_p = pltpu.make_async_copy(p_hbm, pv, local_sem.at[0])
    load_p.start()
    load_c = pltpu.make_async_copy(c_hbm, cv.at[0], local_sem.at[1])
    load_c.start()

    peers = [at_x(xr), at_x(xl), at_x(xo), at_y(yr), at_y(yl), at_y(yo), partner]
    peers += [at_z(zat(d)) for d in range(1, NZ)]
    barrier = pltpu.get_barrier_semaphore()
    for peer in peers:
        pl.semaphore_signal(barrier, inc=1, device_id=peer, device_id_type=MESH_ID)
    pl.semaphore_wait(barrier, len(peers))

    def slot(s):
        return pl.ds(s * 512, 512)

    def cols(f):
        return pl.ds(pl.multiple_of(f * FEATS, FEATS), FEATS)

    ids[:, slot(0)] = jnp.where(keep_ref[...] > 0, assign_ref[...], -1)
    load_p.wait()
    lo, hi = pl.ds(0, 256), pl.ds(256, 256)
    relay_l = remote(pv.at[lo, cols(xo)], relay.at[0], at_x(xr))
    relay_r = remote(pv.at[hi, cols(xo)], relay.at[1], at_x(xl))
    from_l = remote(pv.at[:, cols(xr)], near.at[slot(2)], at_x(xr))
    from_r = remote(pv.at[:, cols(xl)], near.at[slot(3)], at_x(xl))
    own = pltpu.make_async_copy(pv.at[:, cols(x)], near.at[slot(0)], local_sem.at[2])
    own.start()
    from_p = remote(pv.at[:, cols(x)], near.at[slot(1)], partner)
    i_p = remote(ids.at[:, slot(0)], ids.at[:, slot(1)], partner)
    i_l = remote(ids.at[:, slot(0)], ids.at[:, slot(2)], at_x(xr))
    i_r = remote(ids.at[:, slot(0)], ids.at[:, slot(3)], at_x(xl))
    i_o = remote(ids.at[:, slot(0)], ids.at[:, slot(6)], at_x(xo))
    c_p = remote(c_hbm, cv.at[1], partner)

    best[...] = jnp.full(best.shape, jnp.inf, jnp.float32)

    def distances(s):
        def tile(t, carry):
            part = cv[s, pl.ds(pl.multiple_of(t * TILE, TILE), TILE), :]
            inner = lax.dot_general(
                part, pv[...], (((1,), (1,)), ((), ())), preferred_element_type=jnp.float32
            )
            wide = part.astype(jnp.float32)
            square = jnp.sum(wide * wide, axis=1, keepdims=True)
            dist = square - 2.0 * inner
            low = jnp.min(dist.reshape(TILE // 8, 8, 512), axis=0)
            best[...] = jnp.minimum(best[...], low)
            return carry

        lax.fori_loop(0, 2048 // TILE, tile, 0)

    def accumulate(pair, yc, first=False):
        where = pl.ds(pair * 1024, 1024)
        base = m * 2048 + yc * CROWS

        def tile(t, carry):
            rows = pl.ds(pl.multiple_of(t * TILE, TILE), TILE)
            at = lax.broadcasted_iota(jnp.int32, (TILE, 1024), 0)
            hit = jnp.where(at == ids[:, where] - (base + t * TILE), 1.0, 0.0)
            part = jnp.dot(hit.astype(jnp.bfloat16), near[where, :], preferred_element_type=jnp.float32)
            count = sum(hit[:, k * LANES : (k + 1) * LANES] for k in range(1024 // LANES))
            if first:
                acc[yc, rows, :] = part
                cnt[yc, rows, :] = count
            else:
                acc[yc, rows, :] += part
                cnt[yc, rows, :] += count
            return carry

        lax.fori_loop(0, CROWS // TILE, tile, 0)

    def accumulate_all(pair, first=False):
        def body(yc, carry):
            accumulate(pair, yc, first)
            return carry

        lax.fori_loop(0, NY, body, 0)

    load_c.wait()
    distances(0)
    own.wait()
    from_p.wait_recv()
    i_p.wait_recv()
    accumulate_all(0, True)
    relay_l.wait_recv()
    on_l = remote(relay.at[0], near.at[pl.ds(6 * 512, 256)], at_x(xr))
    relay_r.wait_recv()
    on_r = remote(relay.at[1], near.at[pl.ds(6 * 512 + 256, 256)], at_x(xl))
    c_p.wait_recv()
    distances(1)
    from_l.wait_recv()
    i_l.wait_recv()
    p_l = remote(near.at[slot(2)], near.at[slot(4)], partner)
    pi_l = remote(ids.at[:, slot(2)], ids.at[:, slot(4)], partner)
    from_r.wait_recv()
    i_r.wait_recv()
    p_r = remote(near.at[slot(3)], near.at[slot(5)], partner)
    pi_r = remote(ids.at[:, slot(3)], ids.at[:, slot(5)], partner)
    accumulate_all(1)
    p_l.wait_recv()
    pi_l.wait_recv()
    p_r.wait_recv()
    pi_r.wait_recv()
    accumulate_all(2)
    on_l.wait_recv()
    on_r.wait_recv()
    i_o.wait_recv()
    p_o = remote(near.at[slot(6)], near.at[slot(7)], partner)
    pi_o = remote(ids.at[:, slot(6)], ids.at[:, slot(7)], partner)

    eye = lane_eye(LANES)
    for b in range(4):
        part = pv[pl.ds(b * LANES, LANES), :].astype(jnp.float32)
        square = to_row(jnp.sum(part * part, axis=1, keepdims=True), eye)
        lanes = pl.ds(b * LANES, LANES)
        cost_ref[:, lanes] = (square + jnp.min(best[:, lanes], axis=0, keepdims=True)) * (1.0 / 1024)

    p_o.wait_recv()
    pi_o.wait_recv()

    def pack(yc, rows_of, aux, words):
        def block(b, carry):
            eye = lane_eye(LANES)
            rows = pl.ds(pl.multiple_of(b * LANES, LANES), LANES)
            code, step = encode(acc[yc, rows, :])
            words(b, rows, code)
            aux[pl.ds(b, 1), :] = to_row(step, eye)
            if rows_of:
                count = jnp.sum(cnt[yc, rows, :], axis=1, keepdims=True)
                aux[pl.ds(4 + b, 1), :] = to_row(count, eye)
            return carry

        lax.fori_loop(0, CROWS // LANES, block, 0)

    def y_words(k):
        def put(b, rows, code):
            ysend[k, rows, :] = code

        return put

    accumulate(3, yo)
    pack(yo, True, yaux.at[2], y_words(2))
    yrelay_l = remote(ysend.at[2, lo], yrecv.at[3, lo], at_y(yr))
    yrelay_r = remote(ysend.at[2, hi], yrecv.at[3, hi], at_y(yl))
    ya_o = remote(yaux.at[2], yauxr.at[2], at_y(yo))
    accumulate(3, yr)
    pack(yr, True, yaux.at[0], y_words(0))
    y_l = remote(ysend.at[0], yrecv.at[0], at_y(yr))
    ya_l = remote(yaux.at[0], yauxr.at[0], at_y(yr))
    accumulate(3, yl)
    pack(yl, True, yaux.at[1], y_words(1))
    y_r = remote(ysend.at[1], yrecv.at[1], at_y(yl))
    ya_r = remote(yaux.at[1], yauxr.at[1], at_y(yl))
    accumulate(3, y)
    yrelay_l.wait_recv()
    yon_l = remote(yrecv.at[3, lo], yrecv.at[2, lo], at_y(yr))
    yrelay_r.wait_recv()
    yon_r = remote(yrecv.at[3, hi], yrecv.at[2, hi], at_y(yl))

    def unpack(k):
        def block(b, carry):
            eye = lane_eye(LANES)
            rows = pl.ds(pl.multiple_of(b * LANES, LANES), LANES)
            step = to_col(yauxr[k, pl.ds(b, 1), :], eye)
            high, low = decode(yrecv[k, rows, :], step)
            acc[y, rows, :LANES] += high
            acc[y, rows, LANES:] += low
            return carry

        lax.fori_loop(0, CROWS // LANES, block, 0)

    for k, copies in enumerate(((y_l, ya_l), (y_r, ya_r), (yon_l, yon_r, ya_o))):
        for copy in copies:
            copy.wait_recv()
        unpack(k)

    def z_words(b, rows, code):
        zsend[b] = code

    pack(y, True, zaux, z_words)
    zaux[pl.ds(4, 4), :] += yauxr[0, pl.ds(4, 4), :] + yauxr[1, pl.ds(4, 4), :] + yauxr[2, pl.ds(4, 4), :]
    zcopies = {}
    for d in (4, 3, 5, 2, 6, 1, 7):
        to = zat(d)
        piece = zsend.at[to // 2, pl.ds(pl.multiple_of(lax.rem(to, 2) * OWN, OWN), OWN)]
        zcopies[d] = (
            remote(piece, zrecv.at[d - 1], at_z(to)),
            remote(zaux, zauxr.at[d - 1], at_z(to)),
        )
    mine = lane_eye(OWN, lax.rem(z, 2) * OWN)
    zrow = z // 2
    sums = acc[y, pl.ds(pl.multiple_of(z * OWN, OWN), OWN), :]
    first, second = sums[:, :LANES], sums[:, LANES:]
    counts = zaux[pl.ds(4 + zrow, 1), :]
    for d in (1, 7, 2, 6, 3, 5, 4):
        for copy in zcopies[d]:
            copy.wait_recv()
        high, low = decode(zrecv[d - 1], to_col(zauxr[d - 1, pl.ds(zrow, 1), :], mine))
        first, second = first + high, second + low
        counts = counts + zauxr[d - 1, pl.ds(4 + zrow, 1), :]
    count = to_col(counts, mine)
    prior = cv[0, pl.ds(pl.multiple_of((y * NZ + z) * OWN, OWN), OWN), cols(x)].astype(jnp.float32)
    sums = jnp.concatenate([first, second], axis=1)
    fresh = jnp.where(count > 0.5, sums / jnp.maximum(count, 1.0), prior)
    code, step = encode(fresh)
    words_ref[x, y, z] = code
    steps_ref[x, y, z] = to_row(step, lane_eye(OWN))

    bh, ch = pl.ds(0, 32), pl.ds(32, 32)

    class HalfB:
        near_r, near_l, at, up = xr, xl, staticmethod(at_x), True

        @staticmethod
        def first(device):
            return [
                remote(words_ref.at[x, y, z, bh], words_ref.at[x, y, z, bh], device),
                remote(steps_ref.at[x, y, z], steps_ref.at[x, y, z], device),
            ]

        @staticmethod
        def group(along, zc, device):
            return [
                remote(words_ref.at[along, :, zc, bh], words_ref.at[along, :, zc, bh], device),
                remote(steps_ref.at[along, :, zc], steps_ref.at[along, :, zc], device),
            ]

    class HalfC:
        near_r, near_l, at, up = yr, yl, staticmethod(at_y), False

        @staticmethod
        def first(device):
            return [remote(words_ref.at[x, y, z, ch], words_ref.at[x, y, z, ch], device)]

        @staticmethod
        def group(along, zc, device):
            return [remote(words_ref.at[:, along, zc, ch], words_ref.at[:, along, zc, ch], device)]

    def arrive(copies):
        for copy in copies:
            copy.wait_recv()

    halves = (HalfB, HalfC)
    mine_at = {HalfB: x, HalfC: y}
    start = [HalfB.first(at_y(to)) for to in (yo, yr, yl)] + [HalfC.first(at_x(to)) for to in (xo, xr, xl)]
    for copies in start:
        arrive(copies)
    came = {h: {} for h in halves}
    side = {h: {} for h in halves}
    last = {h: {} for h in halves}

    def spread(h, d):
        along, zc = mine_at[h], zat(d)
        side[h][d] = (
            h.group(along, zc, h.at(h.near_r)),
            h.group(along, zc, h.at(h.near_l)),
        )

    def across(h, d):
        zc = zat(d)
        from_left, from_right = side[h][d]
        if d % 2 == 0:
            arrive(from_left)
            last[h][d] = (h.group(h.near_l, zc, h.at(h.near_r)), from_right)
        else:
            arrive(from_right)
            last[h][d] = (h.group(h.near_r, zc, h.at(h.near_l)), from_left)

    for h in halves:
        along = mine_at[h]
        came[h][-1] = h.group(along, z, at_z(zat(1)))
        came[h][1] = h.group(along, z, at_z(zat(-1)))
    for h in halves:
        along = mine_at[h]
        came[h][-2] = h.group(along, z, at_z(zat(2)))
        came[h][2] = h.group(along, z, at_z(zat(-2)))
    for h in halves:
        spread(h, 0)
    for h in halves:
        for d in (-1, 1):
            arrive(came[h][d])
            spread(h, d)
    for h in halves:
        along = mine_at[h]
        for d in (-2, 2):
            arrive(came[h][d])
            step_to = 1 if d < 0 else -1
            came[h][d - step_to] = h.group(along, zat(d), at_z(zat(step_to)))
            spread(h, d)
    for h in halves:
        across(h, 0)
    for h in halves:
        along = mine_at[h]
        for d in (-3, 3):
            arrive(came[h][d])
            if (d < 0) == h.up:
                step_to = 1 if d < 0 else -1
                came[h][4] = h.group(along, zat(d), at_z(zat(step_to)))
            spread(h, d)
    for h in halves:
        for d in (-1, 1):
            across(h, d)
    for h in halves:
        arrive(came[h][4])
        spread(h, 4)
    for h in halves:
        for d in (-2, 2, -3, 3, 4):
            across(h, d)
    for h in halves:
        for d in (0, -1, 1, -2, 2, -3, 3, 4):
            for copies in last[h][d]:
                arrive(copies)
    for copy in used:
        copy.wait_send()
    assert len(used) == N_COPIES, len(used)


N_COPIES = 143


def decode_kernel(words_ref, steps_ref, out_ref):
    eye = lane_eye(OWN)
    for xc in range(NX):
        for zc in range(NZ):
            step = to_col(steps_ref[xc, 0, zc], eye)
            high, low = decode(words_ref[xc, 0, zc], step)
            rows = pl.ds(zc * OWN, OWN)
            out_ref[rows, xc * FEATS : xc * FEATS + LANES] = high
            out_ref[rows, xc * FEATS + LANES : (xc + 1) * FEATS] = low


def shards(points, centroids, assign, keep_mask):
    vmem = pl.BlockSpec(memory_space=pltpu.VMEM)
    anywhere = pl.BlockSpec(memory_space=pl.ANY)
    dma = pltpu.SemaphoreType.DMA
    f32, i32, bf16 = jnp.float32, jnp.int32, jnp.bfloat16
    words, steps, cost = pl.pallas_call(
        update_kernel,
        out_shape=(
            jax.ShapeDtypeStruct((NX, NY, NZ, OWN, LANES), i32),
            jax.ShapeDtypeStruct((NX, NY, NZ, 1, LANES), f32),
            jax.ShapeDtypeStruct((1, 512), f32),
        ),
        in_specs=[anywhere, anywhere, vmem, vmem],
        out_specs=(vmem, vmem, vmem),
        scratch_shapes=[
            pltpu.VMEM((512, 1024), bf16),
            pltpu.VMEM((2, 2048, 1024), bf16),
            pltpu.VMEM((4096, FEATS), bf16),
            pltpu.VMEM((1, 4096), i32),
            pltpu.VMEM((2, 256, FEATS), bf16),
            pltpu.VMEM((8, 512), f32),
            pltpu.VMEM((NY, CROWS, FEATS), f32),
            pltpu.VMEM((NY, CROWS, LANES), f32),
            pltpu.VMEM((3, CROWS, LANES), i32),
            pltpu.VMEM((3, 8, LANES), f32),
            pltpu.VMEM((4, CROWS, LANES), i32),
            pltpu.VMEM((3, 8, LANES), f32),
            pltpu.VMEM((4, LANES, LANES), i32),
            pltpu.VMEM((8, LANES), f32),
            pltpu.VMEM((NZ - 1, OWN, LANES), i32),
            pltpu.VMEM((NZ - 1, 8, LANES), f32),
            dma((N_COPIES,)), dma((N_COPIES,)), dma((3,)),
        ],
        compiler_params=pltpu.CompilerParams(
            collective_id=0, has_side_effects=True, vmem_limit_bytes=48 * 1024 * 1024
        ),
    )(points, centroids, assign.reshape(1, 512), keep_mask.reshape(1, 512))
    new_centroids = pl.pallas_call(
        decode_kernel,
        grid=(NY,),
        out_shape=jax.ShapeDtypeStruct((2048, 1024), f32),
        in_specs=[
            pl.BlockSpec((NX, 1, NZ, OWN, LANES), lambda i: (0, i, 0, 0, 0)),
            pl.BlockSpec((NX, 1, NZ, 1, LANES), lambda i: (0, i, 0, 0, 0)),
        ],
        out_specs=pl.BlockSpec((CROWS, 1024), lambda i: (i, 0)),
        cost_estimate=pl.CostEstimate(flops=8 << 20, bytes_accessed=12 << 20, transcendentals=0),
    )(words, steps)
    return new_centroids, cost.reshape(512)


def solution(mesh):
    grid = Mesh(mesh.devices.reshape(NZ, NY, NX, 2), ("z", "y", "x", "mp"))
    rows = ("z", "y", "x", "mp")
    in_specs = (P(rows, None), P("mp", None), P(rows), P(rows))
    out_specs = (P("mp", None), P(rows))
    return jax.shard_map(shards, mesh=grid, in_specs=in_specs, out_specs=out_specs, check_vma=False)
```

time: 314 us -> 99 us (0.32)
  Pallas kernels: 273 us -> 91.9 us
  other arithmetic: 15.1 us -> 0 us
  between operations: 14.1 us -> 0.66 us
  matrix products: 5.07 us -> 0 us
    pallas_call x1 -> x2, Pallas kernels: 273 us -> 91.9 us  [the longest x1 85.5 us: shards(): pl.pallas_call(update_kernel, out_shape=(jax.ShapeDtypeStruct((NX, NY, NZ...]
    reduce_sum x2 -> x0, other arithmetic: 5.52 us -> none  [the longest x1 5.24 us: shards(): cent_sq = jnp.sum(piece_f * piece_f, axis=1)]
    dot_general x1 -> x0, matrix products: 5.07 us -> none  [shards(): lax.dot_general(points, piece, (((1,), (1,)), ((), ())), preferred_elemen...]
    unnamed x6 -> x11, local copies, waits for them, and re-layouts: 1.76 us -> 5.7 us
    mul x1 -> x0, other arithmetic: 3.78 us -> none  [shards(): pair.astype(jnp.float32) * scale]
    shift_right_arithmetic x1 -> x0, other arithmetic: 3.27 us -> none  [shards(): pair = jnp.concatenate([codes >> 16, codes << 16 >> 16], axis=2)]
  transfers between devices with their start and end apart: 1 -> 0, of which waited for: 0 -> 0; matrix products, arithmetic and copies ran while one was open for 3% -> 0% of each run, Pallas kernels for 88% -> 0%
where the time goes in v1:
time: 99 us; the launch traced here: 98.3 us
  Pallas kernels  91.9 us (93%)
  local copies, waits for them, and re-layouts  5.7 us (6%)
    pallas_call x1, Pallas kernels, shards(): pl.pallas_call(update_kernel, out_shape=(jax.ShapeDtypeStruct((NX, NY, NZ...  85.5 us
    pallas_call x1, Pallas kernels, shards(): pl.pallas_call(decode_kernel, grid=(NY,), out_shape=jax.ShapeDtypeStruct(...  6.4 us
    unnamed x11, local copies, waits for them, and re-layouts  5.7 us

profile of v1, /device:TPU:2, one launch (start us, length us, event | category | flops | bytes accessed | tf_op | source)
XLA Modules:
  0.0 98.3 jit_solution(9860040367058224844)
XLA Ops:
  0.6 0.0 copy-start.1
  0.6 1.2 %copy-done.1 = bf16[512,1024]{1,0:T(8,128)(2,1)S(1)} copy-done((bf16[512,1024]{1,0:T(8,128)(2,1)S(1)}, bf16[512,1024]{1,0:T(8,128)(2,1)}, u32[]{:S(2)}) %copy-start.1) | copy-done | bytes 1048600
  1.9 0.0 copy-start.3
  1.9 0.7 copy-done.3
  2.5 0.0 copy-start.4
  2.5 0.7 copy-done.4
  3.2 85.5 %shard_map.59 = (s32[4,4,8,64,128]{4,3,2,1,0:T(8,128)S(1)}, f32[4,4,8,1,128]{4,3,2,1,0:T(1,128)S(1)}, f32[1,512]{1,0:T(1,128)S(1)}) custom-call(bf16[512,1024]{1,0:T(8,128)(2,1)S(1)} %copy-done.1, bf16[2048,1024]{1,0:T(8,128)(2,1)} %c_hbm.1, s32[1,512]{1,0:T(1,128)S(1)} %bitcast.3, s32[1,512]{1,0:T(1,128)S(1)} %bitcast.4), custom_call_target="tpu_custom_call" | custom-call | tf_op jit(solution)/shard_map/pallas_call | solution.py:410
  88.7 0.0 copy-start
  88.8 1.9 %copy-done = s32[4,4,8,64,128]{4,3,2,1,0:T(8,128)} copy-done((s32[4,4,8,64,128]{4,3,2,1,0:T(8,128)}, s32[4,4,8,64,128]{4,3,2,1,0:T(8,128)S(1)}, u32[]{:S(2)}) %copy-start) | copy-done | bytes 4194328
  90.7 0.0 copy-start.2
  90.7 0.6 copy-done.2
  91.3 6.4 %shard_map.60 = f32[2048,1024]{1,0:T(8,128)} custom-call(s32[4,4,8,64,128]{4,3,2,1,0:T(8,128)} %copy-done, f32[4,4,8,1,128]{4,3,2,1,0:T(1,128)} %copy-done.2), custom_call_target="tpu_custom_call" | custom-call | flops 8388608 | bytes 12582912 | tf_op jit(solution)/shard_map/pallas_call | solution.py:442
  97.7 0.6 copy.7
Async XLA Ops:
  0.6 1.2 %copy-start.1 = (bf16[512,1024]{1,0:T(8,128)(2,1)S(1)}, bf16[512,1024]{1,0:T(8,128)(2,1)}, u32[]{:S(2)}) copy-start(bf16[512,1024]{1,0:T(8,128)(2,1)} %p_hbm.1) | copy-start | bytes 3145732
  1.9 0.7 copy-start.3
  2.5 0.7 copy-start.4
  88.7 1.9 %copy-start = (s32[4,4,8,64,128]{4,3,2,1,0:T(8,128)}, s32[4,4,8,64,128]{4,3,2,1,0:T(8,128)S(1)}, u32[]{:S(2)}) copy-start(s32[4,4,8,64,128]{4,3,2,1,0:T(8,128)S(1)} %get-tuple-element.5.words_ref) | copy-start | bytes 12582916
  90.7 0.6 copy-start.2

commit v2 on v0

v2 whole, which is shorter than its diff:
```python
import jax
import jax.numpy as jnp
from jax import lax
from jax.experimental import pallas as pl
from jax.experimental.pallas import tpu as pltpu
from jax.sharding import Mesh
from jax.sharding import PartitionSpec as P

STEPS = 32000.0
TINY = 2.0**-100
N, NZ = 4, 8
LANES = 128
CROWS = 512
OWN = 64
PAIRS = OWN // 2
TILE = 256
ROWS = 512
MESH_ID = pl.DeviceIdType.MESH


def encode(v):
    top = jnp.maximum(jnp.max(jnp.abs(v), axis=1, keepdims=True), TINY)
    code = jnp.floor(v * (STEPS / top) + 0.5).astype(jnp.int32)
    return code, top * (1.0 / STEPS)


def pair(code):
    return (code[:PAIRS] << 16) | (code[PAIRS:] & 0xFFFF)


def decode(words, step):
    high = (words >> 16).astype(jnp.float32)
    low = ((words << 16) >> 16).astype(jnp.float32)
    return high * step[:PAIRS], low * step[PAIRS:]


def lane_eye(rows, shift=0):
    at_row = lax.broadcasted_iota(jnp.int32, (rows, LANES), 0)
    at_lane = lax.broadcasted_iota(jnp.int32, (rows, LANES), 1)
    return at_lane == at_row + shift


def to_row(col, eye):
    return jnp.sum(jnp.where(eye, col, 0.0), axis=0, keepdims=True)


def to_col(row, eye):
    return jnp.sum(jnp.where(eye, row, 0.0), axis=1, keepdims=True)


def update_kernel(
    p_hbm, c_hbm, assign_hbm, keep_hbm, words_ref, steps_ref, cost_ref,
    pv, cv, idv, near0, near, ids0, ids, relay, best, acc, cnt,
    ysend, yaux, yrecv, yauxr, zsend, zaux, zrecv, zauxr,
    send_sem, recv_sem, local_sem,
):
    z, y, x, m = (lax.axis_index(n) for n in ("z", "y", "x", "mp"))
    zat = lambda d: lax.rem(z + d + NZ, NZ)
    used = []
    scopes = []

    def phase(name):
        if scopes:
            scopes.pop().__exit__(None, None, None)
        if name:
            scopes.append(jax.named_scope(name))
            scopes[-1].__enter__()

    def remote(src, dst, device):
        k = len(used)
        copy = pltpu.make_async_remote_copy(
            src_ref=src, dst_ref=dst, send_sem=send_sem.at[k], recv_sem=recv_sem.at[k],
            device_id=device, device_id_type=MESH_ID,
        )
        copy.start()
        used.append(copy)
        return copy

    def arrive(copies):
        for copy in copies:
            copy.wait_recv()

    at_x = lambda to: (z, y, to, m)
    at_y = lambda to: (z, to, x, m)
    at_z = lambda to: (to, y, x, m)
    partner = (z, y, x, 1 - m)

    class Colour:
        def __init__(self, c, first, second, at_first, at_second):
            self.c, self.f, self.r = c, first, second
            self.fr, self.fl, self.fo = (lax.rem(first + d, N) for d in (1, 3, 2))
            self.rr, self.rl, self.ro = (lax.rem(second + d, N) for d in (1, 3, 2))
            self.at_f, self.at_r = at_first, at_second

        def cols(self, f):
            return pl.ds(pl.multiple_of(self.c * 512 + f * LANES, LANES), LANES)

    colours = (Colour(0, x, y, at_x, at_y), Colour(1, y, x, at_y, at_x))

    phase("enter")
    loads = [
        pltpu.make_async_copy(p_hbm, pv, local_sem.at[0]),
        pltpu.make_async_copy(assign_hbm, idv.at[0], local_sem.at[1]),
        pltpu.make_async_copy(keep_hbm, idv.at[1], local_sem.at[2]),
    ]
    load_c = pltpu.make_async_copy(c_hbm, cv.at[0], local_sem.at[3])
    for copy in loads + [load_c]:
        copy.start()

    peers = [partner] + [at_z(zat(d)) for d in range(1, NZ)]
    for k in colours:
        peers += [k.at_f(k.fr), k.at_f(k.fl), k.at_f(k.fo)]
    barrier = pltpu.get_barrier_semaphore()
    for peer in peers:
        pl.semaphore_signal(barrier, inc=1, device_id=peer, device_id_type=MESH_ID)
    for copy in loads:
        copy.wait()
    ids0[:, :ROWS] = jnp.where(idv[1] > 0, idv[0], -1)
    best[...] = jnp.full(best.shape, jnp.inf, jnp.float32)
    pl.semaphore_wait(barrier, len(peers))

    phase("send_p")

    def slot(s):
        return pl.ds((s - 2) * ROWS, ROWS)

    lo, hi = pl.ds(0, ROWS // 2), pl.ds(ROWS // 2, ROWS // 2)
    mine_ids = ids0.at[:, pl.ds(0, ROWS)]
    for k in colours:
        k.relay_l = remote(pv.at[lo, k.cols(k.fo)], relay.at[k.c, 0], k.at_f(k.fr))
        k.relay_r = remote(pv.at[hi, k.cols(k.fo)], relay.at[k.c, 1], k.at_f(k.fl))
    own = []
    from_p = [remote(mine_ids, ids0.at[:, pl.ds(ROWS, ROWS)], partner)]
    for k in colours:
        lanes = pl.ds(k.c * LANES, LANES)
        own.append(
            pltpu.make_async_copy(pv.at[:, k.cols(k.f)], near0.at[pl.ds(0, ROWS), lanes], local_sem.at[4 + k.c])
        )
        own[-1].start()
        from_p.append(remote(pv.at[:, k.cols(k.f)], near0.at[pl.ds(ROWS, ROWS), lanes], partner))
    for k in colours:
        k.from_l = [
            remote(mine_ids, ids.at[k.c, :, slot(2)], k.at_f(k.fr)),
            remote(pv.at[:, k.cols(k.fr)], near.at[k.c, slot(2)], k.at_f(k.fr)),
        ]
        k.from_r = [
            remote(mine_ids, ids.at[k.c, :, slot(3)], k.at_f(k.fl)),
            remote(pv.at[:, k.cols(k.fl)], near.at[k.c, slot(3)], k.at_f(k.fl)),
        ]
        k.from_o = [remote(mine_ids, ids.at[k.c, :, slot(6)], k.at_f(k.fo))]
    c_p = remote(c_hbm, cv.at[1], partner)

    def distances(s, first, count):
        def tile(t, carry):
            part = cv[s, pl.ds(pl.multiple_of(t * TILE, TILE), TILE), :]
            inner = lax.dot_general(
                part, pv[...], (((1,), (1,)), ((), ())), preferred_element_type=jnp.float32
            )
            wide = part.astype(jnp.float32)
            square = jnp.sum(wide * wide, axis=1, keepdims=True)
            dist = square - 2.0 * inner
            low = jnp.min(dist.reshape(TILE // 8, 8, ROWS), axis=0)
            best[...] = jnp.minimum(best[...], low)
            return carry

        lax.fori_loop(first, first + count, tile, 0)

    def hits(id_row, base):
        local = id_row - base
        local = jnp.where((local >= 0) & (local < TILE), local, -1).astype(jnp.float32)
        local = jnp.broadcast_to(local, (16, 2 * ROWS)).astype(jnp.bfloat16)
        at = lax.broadcasted_iota(jnp.int32, (TILE, LANES), 0).astype(jnp.float32).astype(jnp.bfloat16)
        at = at.reshape(TILE // 16, 16, LANES)
        one, zero = jnp.ones((), jnp.bfloat16), jnp.zeros((), jnp.bfloat16)
        parts = [
            jnp.where(at == local[None, :, i * LANES : (i + 1) * LANES], one, zero).reshape(TILE, LANES)
            for i in range(2 * ROWS // LANES)
        ]
        count = parts[0]
        for part in parts[1:]:
            count = count + part
        return jnp.concatenate(parts, axis=1), count

    def accumulate(k, two, q):
        where = pl.ds((two - 1) * 2 * ROWS, 2 * ROWS)

        def tile(t, carry):
            rows = pl.ds(pl.multiple_of(t * TILE, TILE), TILE)
            hit, count = hits(ids[k.c, :, where], m * 2048 + q * CROWS + t * TILE)
            acc[k.c, q, rows, :] += jnp.dot(hit, near[k.c, where, :], preferred_element_type=jnp.float32)
            cnt[k.c, q, rows, :] += count
            return carry

        lax.fori_loop(0, CROWS // TILE, tile, 0)

    def accumulate_all(k, two):
        def body(q, carry):
            accumulate(k, two, q)
            return carry

        lax.fori_loop(0, N, body, 0)

    def accumulate_own():
        def tile(t, carry):
            q, rows = t // 2, pl.ds(pl.multiple_of(lax.rem(t, 2) * TILE, TILE), TILE)
            hit, count = hits(ids0[...], m * 2048 + t * TILE)
            part = jnp.dot(hit, near0[...], preferred_element_type=jnp.float32)
            for c in range(2):
                acc[c, q, rows, :] = part[:, c * LANES : (c + 1) * LANES]
                cnt[c, q, rows, :] = count
            return carry

        lax.fori_loop(0, 2048 // TILE, tile, 0)

    phase("dist0a")
    load_c.wait()
    distances(0, 0, 4)
    phase("w_own")
    for copy in own:
        copy.wait()
    arrive(from_p)
    phase("acc0")
    accumulate_own()
    phase("w_relay")
    for k in colours:
        k.relay_l.wait_recv()
        k.from_o.append(remote(relay.at[k.c, 0], near.at[k.c, pl.ds(4 * ROWS, ROWS // 2)], k.at_f(k.fr)))
        k.relay_r.wait_recv()
        k.from_o.append(remote(relay.at[k.c, 1], near.at[k.c, pl.ds(4 * ROWS + ROWS // 2, ROWS // 2)], k.at_f(k.fl)))
    phase("dist0b")
    distances(0, 4, 4)

    def to_partner(k, source, target):
        return [
            remote(near.at[k.c, slot(source)], near.at[k.c, slot(target)], partner),
            remote(ids.at[k.c, :, slot(source)], ids.at[k.c, :, slot(target)], partner),
        ]

    phase("w_lr")
    for k in colours:
        arrive(k.from_l)
        k.two = to_partner(k, 2, 4)
        arrive(k.from_r)
        k.two += to_partner(k, 3, 5)
    phase("acc1")
    accumulate_all(colours[0], 1)
    phase("w_o")
    for k in colours:
        arrive(k.from_o)
        k.three = to_partner(k, 6, 7)
    phase("acc1b")
    accumulate_all(colours[1], 1)
    phase("w_plr")
    for k in colours:
        arrive(k.two)
    phase("acc2")
    for k in colours:
        accumulate_all(k, 2)
    phase("w_po")
    for k in colours:
        arrive(k.three)

    def pack(c, q, words, aux):
        def block(b, carry):
            eye = lane_eye(LANES)
            rows = pl.ds(pl.multiple_of(b * LANES, LANES), LANES)
            code, step = encode(acc[c, q, rows, :])
            for j in range(2):
                words(2 * b + j)[...] = pair(code[j * OWN : (j + 1) * OWN])
            count = jnp.sum(cnt[c, q, rows, :].astype(jnp.float32), axis=1, keepdims=True)
            aux(b, to_row(step, eye), to_row(count, eye))
            return carry

        lax.fori_loop(0, CROWS // LANES, block, 0)

    def pack_y(k, q, s):
        def aux(b, step, count):
            yaux[k.c, s, b, 0:1, :] = step
            yaux[k.c, s, b, 1:2, :] = count

        accumulate(k, 3, q)
        pack(k.c, q, lambda zb: ysend.at[k.c, s, zb], aux)

    h0, h1 = pl.ds(0, NZ // 2), pl.ds(NZ // 2, NZ // 2)
    phase("y_pack")
    for k in colours:
        pack_y(k, k.ro, 2)
        k.yrelay_l = remote(ysend.at[k.c, 2, h0], yrecv.at[k.c, 3, h0], k.at_r(k.rr))
        k.yrelay_r = remote(ysend.at[k.c, 2, h1], yrecv.at[k.c, 3, h1], k.at_r(k.rl))
        k.y_o = [remote(yaux.at[k.c, 2], yauxr.at[k.c, 2], k.at_r(k.ro))]
    for k in colours:
        pack_y(k, k.rr, 0)
        k.y_l = [
            remote(yaux.at[k.c, 0], yauxr.at[k.c, 0], k.at_r(k.rr)),
            remote(ysend.at[k.c, 0], yrecv.at[k.c, 0], k.at_r(k.rr)),
        ]
        pack_y(k, k.rl, 1)
        k.y_r = [
            remote(yaux.at[k.c, 1], yauxr.at[k.c, 1], k.at_r(k.rl)),
            remote(ysend.at[k.c, 1], yrecv.at[k.c, 1], k.at_r(k.rl)),
        ]
    phase("y_relay")
    for k in colours:
        k.yrelay_l.wait_recv()
        k.y_o.append(remote(yrecv.at[k.c, 3, h0], yrecv.at[k.c, 2, h0], k.at_r(k.rr)))
        k.yrelay_r.wait_recv()
        k.y_o.append(remote(yrecv.at[k.c, 3, h1], yrecv.at[k.c, 2, h1], k.at_r(k.rl)))
    for k in colours:
        accumulate(k, 3, k.r)

    def unpack(k, s):
        def block(b, carry):
            step = to_col(yauxr[k.c, s, b, 0:1, :], lane_eye(LANES))
            for j in range(2):
                high, low = decode(yrecv[k.c, s, 2 * b + j], step[j * OWN : (j + 1) * OWN])
                base = pl.multiple_of(b * LANES, LANES) + j * OWN
                acc[k.c, k.r, pl.ds(base, PAIRS), :] += high
                acc[k.c, k.r, pl.ds(base + PAIRS, PAIRS), :] += low
            return carry

        lax.fori_loop(0, CROWS // LANES, block, 0)

    phase("y_unpack")
    for k in colours:
        arrive(k.y_l)
        unpack(k, 0)
        arrive(k.y_r)
        unpack(k, 1)
    phase("y_unpack_o")
    for k in colours:
        arrive(k.y_o)
        unpack(k, 2)

    phase("z_pack")
    for k in colours:
        def aux(b, step, count, k=k):
            zaux[b, 2 * k.c : 2 * k.c + 1, :] = step
            for s in range(3):
                count = count + yauxr[k.c, s, b, 1:2, :]
            zaux[b, 2 * k.c + 1 : 2 * k.c + 2, :] = count

        pack(k.c, k.r, lambda zb, k=k: zsend.at[zb, k.c], aux)
    zcopies = {}
    for d in (4, 3, 5, 2, 6, 1, 7):
        to = zat(d)
        zcopies[d] = [
            remote(zaux.at[to // 2], zauxr.at[d - 1], at_z(to)),
            remote(zsend.at[to], zrecv.at[d - 1], at_z(to)),
        ]
    phase("dist1")
    c_p.wait_recv()
    distances(1, 0, 2048 // TILE)
    eye = lane_eye(LANES)
    for b in range(ROWS // LANES):
        part = pv[pl.ds(b * LANES, LANES), :].astype(jnp.float32)
        square = to_row(jnp.sum(part * part, axis=1, keepdims=True), eye)
        lanes = pl.ds(b * LANES, LANES)
        cost_ref[:, lanes] = (square + jnp.min(best[:, lanes], axis=0, keepdims=True)) * (1.0 / 1024)
    phase("z_sum")
    mine = lane_eye(OWN, lax.rem(z, 2) * OWN)
    for k in colours:
        sums = acc[k.c, k.r, pl.ds(pl.multiple_of(z * OWN, OWN), OWN), :]
        k.high, k.low = sums[:PAIRS], sums[PAIRS:]
        k.count = zaux[z // 2, 2 * k.c + 1 : 2 * k.c + 2, :]
    for d in (1, 7, 2, 6, 3, 5, 4):
        arrive(zcopies[d])
        for k in colours:
            step = to_col(zauxr[d - 1, 2 * k.c : 2 * k.c + 1, :], mine)
            high, low = decode(zrecv[d - 1, k.c], step)
            k.high, k.low = k.high + high, k.low + low
            k.count = k.count + zauxr[d - 1, 2 * k.c + 1 : 2 * k.c + 2, :]
    phase("fresh")
    for k in colours:
        count = to_col(k.count, mine)
        rows = pl.ds(pl.multiple_of((k.r * NZ + z) * OWN, OWN), OWN)
        prior = cv[0, rows, k.cols(k.f)].astype(jnp.float32)
        sums = jnp.concatenate([k.high, k.low], axis=0)
        code, step = encode(jnp.where(count > 0.5, sums / jnp.maximum(count, 1.0), prior))
        words_ref[k.c, k.f, k.r, z] = pair(code)
        steps_ref[k.c, k.f, k.r, z] = to_row(step, lane_eye(OWN))
        k.start = []
        for to in (k.ro, k.rr, k.rl):
            for ref in (steps_ref, words_ref):
                own_piece = ref.at[k.c, k.f, k.r, z]
                k.start.append(remote(own_piece, own_piece, k.at_r(to)))

    def group(k, f, zc, device):
        copies = []
        for ref in (steps_ref, words_ref):
            piece = ref.at[k.c, f, :, zc]
            copies.append(remote(piece, piece, device))
        return copies

    def hop(k, way, h, half):
        zc, device = zat(-way * (h - 1)), at_z(zat(way))
        copies = []
        if half == 0:
            piece = steps_ref.at[k.c, k.f, :, zc]
            copies.append(remote(piece, piece, device))
        piece = words_ref.at[k.c, k.f, pl.ds(half * (N // 2), N // 2), zc]
        copies.append(remote(piece, piece, device))
        k.hops[way, h, half] = copies

    def spread(k, d):
        zc = zat(d)
        k.side[d] = (group(k, k.f, zc, k.at_f(k.fr)), group(k, k.f, zc, k.at_f(k.fl)))

    def across(k, d):
        zc = zat(d)
        from_left, from_right = k.side[d]
        if d in (0, 1, 2, 3):
            arrive(from_left)
            k.last += group(k, k.fl, zc, k.at_f(k.fr)) + from_right
        else:
            arrive(from_right)
            k.last += group(k, k.fr, zc, k.at_f(k.fl)) + from_left

    phase("g1")
    for k in colours:
        arrive(k.start)
        k.hops, k.side, k.last = {}, {}, []
        for half in (0, 1):
            for way in (1, -1):
                hop(k, way, 1, half)
        spread(k, 0)
    for h in (1, 2, 3):
        phase(f"g_z{h}")
        for k in colours:
            for half in (0, 1):
                for way in (1, -1):
                    arrive(k.hops[way, h, half])
                    if h < 3 or way == (1, -1)[half]:
                        hop(k, way, h + 1, half)
            for way in (1, -1):
                spread(k, -way * h)
        phase(f"g_x{h}")
        for k in colours:
            for d in (0,) if h == 1 else (1 - h, h - 1):
                across(k, d)
    phase("g_z4")
    for k in colours:
        arrive(k.hops[1, 4, 0])
        arrive(k.hops[-1, 4, 1])
        spread(k, 4)
    phase("g_x4")
    for k in colours:
        for d in (-3, 3, 4):
            across(k, d)
    phase("g_last")
    for k in colours:
        arrive(k.last)
    phase("w_send")
    for copy in used:
        copy.wait_send()
    phase(None)
    assert len(used) == N_COPIES, len(used)


N_COPIES = 216


def decode_kernel(words_ref, steps_ref, cost_ref, out_hbm, cost_hbm, rows_ref, sems):
    put_cost = pltpu.make_async_copy(cost_ref, cost_hbm, sems.at[N])
    put_cost.start()
    puts = []
    for r in range(N):

        def block(zb, carry):
            eye = lane_eye(OWN)
            base = pl.multiple_of(zb * OWN, OWN)
            for c in range(2):
                for f in range(N):
                    step = to_col(steps_ref[c, f, r, zb], eye)
                    high, low = decode(words_ref[c, f, r, zb], step)
                    lanes = pl.ds((c * N + f) * LANES, LANES)
                    rows_ref[r, pl.ds(base, PAIRS), lanes] = high
                    rows_ref[r, pl.ds(base + PAIRS, PAIRS), lanes] = low
            return carry

        lax.fori_loop(0, NZ, block, 0)
        put = pltpu.make_async_copy(rows_ref.at[r], out_hbm.at[pl.ds(r * CROWS, CROWS)], sems.at[r])
        put.start()
        puts.append(put)
    for put in puts + [put_cost]:
        put.wait()


def shards(points, centroids, assign, keep_mask):
    vmem = pl.BlockSpec(memory_space=pltpu.VMEM)
    hbm = pl.BlockSpec(memory_space=pltpu.HBM)
    dma = pltpu.SemaphoreType.DMA
    f32, i32, bf16 = jnp.float32, jnp.int32, jnp.bfloat16
    args = (points, centroids, assign.reshape(1, ROWS), keep_mask.reshape(1, ROWS))
    words, steps, cost = pl.pallas_call(
        update_kernel,
        out_shape=(
            jax.ShapeDtypeStruct((2, N, N, NZ, PAIRS, LANES), i32),
            jax.ShapeDtypeStruct((2, N, N, NZ, 1, LANES), f32),
            jax.ShapeDtypeStruct((1, ROWS), f32),
        ),
        in_specs=[hbm] * 4,
        out_specs=(vmem, vmem, vmem),
        scratch_shapes=[
            pltpu.VMEM((ROWS, 1024), bf16),
            pltpu.VMEM((2, 2048, 1024), bf16),
            pltpu.VMEM((2, 1, ROWS), i32),
            pltpu.VMEM((2 * ROWS, 2 * LANES), bf16),
            pltpu.VMEM((2, 6 * ROWS, LANES), bf16),
            pltpu.VMEM((1, 2 * ROWS), i32),
            pltpu.VMEM((2, 1, 6 * ROWS), i32),
            pltpu.VMEM((2, 2, ROWS // 2, LANES), bf16),
            pltpu.VMEM((8, ROWS), f32),
            pltpu.VMEM((2, N, CROWS, LANES), f32),
            pltpu.VMEM((2, N, CROWS, LANES), bf16),
            pltpu.VMEM((2, 3, NZ, PAIRS, LANES), i32),
            pltpu.VMEM((2, 3, N, 2, LANES), f32),
            pltpu.VMEM((2, 4, NZ, PAIRS, LANES), i32),
            pltpu.VMEM((2, 3, N, 2, LANES), f32),
            pltpu.VMEM((NZ, 2, PAIRS, LANES), i32),
            pltpu.VMEM((N, 4, LANES), f32),
            pltpu.VMEM((NZ - 1, 2, PAIRS, LANES), i32),
            pltpu.VMEM((NZ - 1, 4, LANES), f32),
            dma((N_COPIES,)), dma((N_COPIES,)), dma((6,)),
        ],
        compiler_params=pltpu.CompilerParams(
            collective_id=0, has_side_effects=True, vmem_limit_bytes=40 * 1024 * 1024
        ),
    )(*(pltpu.with_memory_space_constraint(a, pltpu.HBM) for a in args))
    new_centroids, cost = pl.pallas_call(
        decode_kernel,
        out_shape=(jax.ShapeDtypeStruct((2048, 1024), f32), jax.ShapeDtypeStruct((1, ROWS), f32)),
        in_specs=[vmem] * 3,
        out_specs=(hbm, hbm),
        scratch_shapes=[pltpu.VMEM((N, CROWS, 1024), f32), dma((N + 1,))],
        compiler_params=pltpu.CompilerParams(vmem_limit_bytes=12 * 1024 * 1024),
        cost_estimate=pl.CostEstimate(flops=8 << 20, bytes_accessed=12 << 20, transcendentals=0),
    )(words, steps, cost)
    return new_centroids, cost.reshape(ROWS)


def solution(mesh):
    grid = Mesh(mesh.devices.reshape(NZ, N, N, 2), ("z", "y", "x", "mp"))
    rows = ("z", "y", "x", "mp")
    in_specs = (P(rows, None), P("mp", None), P(rows), P(rows))
    out_specs = (P("mp", None), P(rows))
    return jax.shard_map(shards, mesh=grid, in_specs=in_specs, out_specs=out_specs, check_vma=False)
```

time: 314 us -> 84.6 us (0.27); the launches traced: 310 us -> 84.3 us
  Pallas kernels: 273 us -> 83.7 us
  other arithmetic: 15.1 us -> 0 us
  between operations: 14.1 us -> 0.64 us
  matrix products: 5.07 us -> 0 us
    pallas_call x1 -> x2, Pallas kernels: 273 us -> 83.7 us  [the longest x1 77.7 us: shards(): pl.pallas_call(update_kernel, out_shape=(jax.ShapeDtypeStruct((2, N, N, N...]
    reduce_sum x2 -> x0, other arithmetic: 5.52 us -> none  [the longest x1 5.24 us: shards(): cent_sq = jnp.sum(piece_f * piece_f, axis=1)]
    dot_general x1 -> x0, matrix products: 5.07 us -> none  [shards(): lax.dot_general(points, piece, (((1,), (1,)), ((), ())), preferred_elemen...]
    mul x1 -> x0, other arithmetic: 3.78 us -> none  [shards(): pair.astype(jnp.float32) * scale]
    shift_right_arithmetic x1 -> x0, other arithmetic: 3.27 us -> none  [shards(): pair = jnp.concatenate([codes >> 16, codes << 16 >> 16], axis=2)]
  transfers between devices with their start and end apart: 1 -> 0, of which waited for: 0 -> 0; matrix products, arithmetic and copies ran while one was open for 3% -> 0% of each run, Pallas kernels for 88% -> 0%
where the time goes in v2:
time: 84.6 us; the launch traced here: 84.3 us
  Pallas kernels  83.7 us (99%)
    pallas_call x1, Pallas kernels, shards(): pl.pallas_call(update_kernel, out_shape=(jax.ShapeDtypeStruct((2, N, N, N...  77.7 us
    pallas_call x1, Pallas kernels, shards(): pl.pallas_call(decode_kernel, out_shape=(jax.ShapeDtypeStruct((2048, 1024...  5.96 us

profile of v2, /device:TPU:2, one launch (start us, length us, event | category | flops | bytes accessed | tf_op | source)
XLA Modules:
  0.0 84.3 jit_solution(13817305441137478137)
XLA Ops:
  0.6 77.7 %shard_map.59 = (s32[2,4,4,8,32,128]{5,4,3,2,1,0:T(8,128)S(1)}, f32[2,4,4,8,1,128]{5,4,3,2,1,0:T(1,128)S(1)}, f32[1,512]{1,0:T(1,128)S(1)}) custom-call(bf16[512,1024]{1,0:T(8,128)(2,1)} %p_hbm.1, bf16[2048,1024]{1,0:T(8,128)(2,1)} %c_hbm.1, s32[1,512]{1,0:T(1,128)} %bitcast.3, s32[1,512]{1,0:T(1,128)} %bitcast.4), custom_call_target="tpu_custom_call" | custom-call | tf_op jit(solution)/shard_map/pallas_call | solution.py:494
  78.3 6.0 %shard_map.60 = (f32[2048,1024]{1,0:T(8,128)}, f32[1,512]{1,0:T(1,128)}) custom-call(s32[2,4,4,8,32,128]{5,4,3,2,1,0:T(8,128)S(1)} %get-tuple-element.7.words_ref, f32[2,4,4,8,1,128]{5,4,3,2,1,0:T(1,128)S(1)} %get-tuple-element.8.steps_ref, f32[1,512]{1,0:T(1,128)S(1)} %get-tuple-element.9.cost_ref), custom_call_target="tpu_custom_call" | custom-call | flops 8388608 | bytes 12582912 | tf_op jit(solution)/shard_map/pallas_call | solution.py:529

commit v3 on v2

--- a/solution.py
+++ b/solution.py
@@ -49,7 +49,8 @@
 
 
 def update_kernel(
-    p_hbm, c_hbm, assign_hbm, keep_hbm, words_ref, steps_ref, cost_ref,
+    p_hbm, c_hbm, assign_hbm, keep_hbm, out_ref, cost_ref,
+    words_ref, steps_ref,
     pv, cv, idv, near0, near, ids0, ids, relay, best, acc, cnt,
     ysend, yaux, yrecv, yauxr, zsend, zaux, zrecv, zauxr,
     send_sem, recv_sem, local_sem,
@@ -181,36 +182,34 @@
             count = count + part
         return jnp.concatenate(parts, axis=1), count
 
-    def accumulate(k, two, q):
+    def hits_chunk(id_row, base):
+        low, count_low = hits(id_row, base)
+        high, count_high = hits(id_row, base + TILE)
+        return jnp.concatenate([low, high], axis=0), jnp.concatenate([count_low, count_high], axis=0)
+
+    def accumulate(c, two, q):
         where = pl.ds((two - 1) * 2 * ROWS, 2 * ROWS)
-
-        def tile(t, carry):
-            rows = pl.ds(pl.multiple_of(t * TILE, TILE), TILE)
-            hit, count = hits(ids[k.c, :, where], m * 2048 + q * CROWS + t * TILE)
-            acc[k.c, q, rows, :] += jnp.dot(hit, near[k.c, where, :], preferred_element_type=jnp.float32)
-            cnt[k.c, q, rows, :] += count
+        hit, count = hits_chunk(ids[c, :, where], m * 2048 + q * CROWS)
+        acc[c, q] += jnp.dot(hit, near[c, where, :], preferred_element_type=jnp.float32)
+        cnt[c, q] += count
+
+    def accumulate_all(c, two):
+        def body(q, carry):
+            accumulate(c, two, q)
             return carry
 
-        lax.fori_loop(0, CROWS // TILE, tile, 0)
-
-    def accumulate_all(k, two):
+        lax.fori_loop(0, N, body, 0)
+
+    def accumulate_own():
         def body(q, carry):
-            accumulate(k, two, q)
-            return carry
-
-        lax.fori_loop(0, N, body, 0)
-
-    def accumulate_own():
-        def tile(t, carry):
-            q, rows = t // 2, pl.ds(pl.multiple_of(lax.rem(t, 2) * TILE, TILE), TILE)
-            hit, count = hits(ids0[...], m * 2048 + t * TILE)
+            hit, count = hits_chunk(ids0[...], m * 2048 + q * CROWS)
             part = jnp.dot(hit, near0[...], preferred_element_type=jnp.float32)
             for c in range(2):
-                acc[c, q, rows, :] = part[:, c * LANES : (c + 1) * LANES]
-                cnt[c, q, rows, :] = count
+                acc[c, q] = part[:, c * LANES : (c + 1) * LANES]
+                cnt[c, q] = count
             return carry
 
-        lax.fori_loop(0, 2048 // TILE, tile, 0)
+        lax.fori_loop(0, N, body, 0)
 
     phase("dist0a")
     load_c.wait()
@@ -243,19 +242,19 @@
         arrive(k.from_r)
         k.two += to_partner(k, 3, 5)
     phase("acc1")
-    accumulate_all(colours[0], 1)
+    accumulate_all(0, 1)
     phase("w_o")
     for k in colours:
         arrive(k.from_o)
         k.three = to_partner(k, 6, 7)
     phase("acc1b")
-    accumulate_all(colours[1], 1)
+    accumulate_all(1, 1)
     phase("w_plr")
     for k in colours:
         arrive(k.two)
     phase("acc2")
     for k in colours:
-        accumulate_all(k, 2)
+        accumulate_all(k.c, 2)
     phase("w_po")
     for k in colours:
         arrive(k.three)
@@ -271,14 +270,14 @@
             aux(b, to_row(step, eye), to_row(count, eye))
             return carry
 
-        lax.fori_loop(0, CROWS // LANES, block, 0)
+        lax.fori_loop(0, CROWS // LANES, block, 0, unroll=True)
 
     def pack_y(k, q, s):
         def aux(b, step, count):
             yaux[k.c, s, b, 0:1, :] = step
             yaux[k.c, s, b, 1:2, :] = count
 
-        accumulate(k, 3, q)
+        accumulate(k.c, 3, q)
         pack(k.c, q, lambda zb: ysend.at[k.c, s, zb], aux)
 
     h0, h1 = pl.ds(0, NZ // 2), pl.ds(NZ // 2, NZ // 2)
@@ -306,7 +305,7 @@
         k.yrelay_r.wait_recv()
         k.y_o.append(remote(yrecv.at[k.c, 3, h1], yrecv.at[k.c, 2, h1], k.at_r(k.rl)))
     for k in colours:
-        accumulate(k, 3, k.r)
+        accumulate(k.c, 3, k.r)
 
     def unpack(k, s):
         def block(b, carry):
@@ -318,7 +317,7 @@
                 acc[k.c, k.r, pl.ds(base + PAIRS, PAIRS), :] += low
             return carry
 
-        lax.fori_loop(0, CROWS // LANES, block, 0)
+        lax.fori_loop(0, CROWS // LANES, block, 0, unroll=True)
 
     phase("y_unpack")
     for k in colours:
@@ -405,50 +404,68 @@
         zc = zat(d)
         k.side[d] = (group(k, k.f, zc, k.at_f(k.fr)), group(k, k.f, zc, k.at_f(k.fl)))
 
+    def left_first(d):
+        return d in (0, 1, 2, 3)
+
     def across(k, d):
         zc = zat(d)
         from_left, from_right = k.side[d]
-        if d in (0, 1, 2, 3):
+        if left_first(d):
             arrive(from_left)
-            k.last += group(k, k.fl, zc, k.at_f(k.fr)) + from_right
+            k.last[d] = (group(k, k.fl, zc, k.at_f(k.fr)), from_right)
         else:
             arrive(from_right)
-            k.last += group(k, k.fr, zc, k.at_f(k.fl)) + from_left
+            k.last[d] = (group(k, k.fr, zc, k.at_f(k.fl)), from_left)
+
+    def finish(groups):
+        def block(r, carry):
+            for k, f, d in groups:
+                zc = zat(d)
+                step = to_col(steps_ref[k.c, f, r, zc], lane_eye(OWN))
+                high, low = decode(words_ref[k.c, f, r, zc], step)
+                base = pl.multiple_of((r * NZ + zc) * OWN, OWN)
+                out_ref[pl.ds(base, PAIRS), k.cols(f)] = high
+                out_ref[pl.ds(base + PAIRS, PAIRS), k.cols(f)] = low
+            return carry
+
+        lax.fori_loop(0, N, block, 0)
 
     phase("g1")
     for k in colours:
         arrive(k.start)
-        k.hops, k.side, k.last = {}, {}, []
+        k.hops, k.side, k.last = {}, {}, {}
         for half in (0, 1):
             for way in (1, -1):
                 hop(k, way, 1, half)
         spread(k, 0)
-    for h in (1, 2, 3):
-        phase(f"g_z{h}")
+    rounds = ((0,), (-1, 1), (-2, 2), (-3, 3), (4,))
+    for h in range(1, 7):
+        if h <= 4:
+            phase(f"g_z{h}")
+            for k in colours:
+                for half in (0, 1):
+                    for way in (1, -1):
+                        if h < 4 or way == (1, -1)[half]:
+                            arrive(k.hops[way, h, half])
+                            if h < 3 or (h == 3 and way == (1, -1)[half]):
+                                hop(k, way, h + 1, half)
+                for d in rounds[h]:
+                    spread(k, d)
+        if h <= 5:
+            phase(f"g_x{h}")
+            for k in colours:
+                for d in rounds[h - 1]:
+                    across(k, d)
+        phase(f"g_f{h}")
+        groups = []
         for k in colours:
-            for half in (0, 1):
-                for way in (1, -1):
-                    arrive(k.hops[way, h, half])
-                    if h < 3 or way == (1, -1)[half]:
-                        hop(k, way, h + 1, half)
-            for way in (1, -1):
-                spread(k, -way * h)
-        phase(f"g_x{h}")
-        for k in colours:
-            for d in (0,) if h == 1 else (1 - h, h - 1):
-                across(k, d)
-    phase("g_z4")
-    for k in colours:
-        arrive(k.hops[1, 4, 0])
-        arrive(k.hops[-1, 4, 1])
-        spread(k, 4)
-    phase("g_x4")
-    for k in colours:
-        for d in (-3, 3, 4):
-            across(k, d)
-    phase("g_last")
-    for k in colours:
-        arrive(k.last)
+            for d in rounds[h - 1] if h <= 5 else ():
+                groups += [(k, k.f, d), (k, k.fl if left_first(d) else k.fr, d)]
+            for d in rounds[h - 2] if h >= 2 else ():
+                for copies in k.last[d]:
+                    arrive(copies)
+                groups += [(k, k.fo, d), (k, k.fr if left_first(d) else k.fl, d)]
+        finish(groups)
     phase("w_send")
     for copy in used:
         copy.wait_send()
@@ -459,29 +476,14 @@
 N_COPIES = 216
 
 
-def decode_kernel(words_ref, steps_ref, cost_ref, out_hbm, cost_hbm, rows_ref, sems):
-    put_cost = pltpu.make_async_copy(cost_ref, cost_hbm, sems.at[N])
-    put_cost.start()
-    puts = []
-    for r in range(N):
-
-        def block(zb, carry):
-            eye = lane_eye(OWN)
-            base = pl.multiple_of(zb * OWN, OWN)
-            for c in range(2):
-                for f in range(N):
-                    step = to_col(steps_ref[c, f, r, zb], eye)
-                    high, low = decode(words_ref[c, f, r, zb], step)
-                    lanes = pl.ds((c * N + f) * LANES, LANES)
-                    rows_ref[r, pl.ds(base, PAIRS), lanes] = high
-                    rows_ref[r, pl.ds(base + PAIRS, PAIRS), lanes] = low
-            return carry
-
-        lax.fori_loop(0, NZ, block, 0)
-        put = pltpu.make_async_copy(rows_ref.at[r], out_hbm.at[pl.ds(r * CROWS, CROWS)], sems.at[r])
+def put_kernel(rows_ref, cost_ref, rows_hbm, cost_hbm, sems):
+    puts = [pltpu.make_async_copy(cost_ref, cost_hbm, sems.at[N])]
+    for q in range(N):
+        rows = pl.ds(q * CROWS, CROWS)
+        puts.append(pltpu.make_async_copy(rows_ref.at[rows], rows_hbm.at[rows], sems.at[q]))
+    for put in puts:
         put.start()
-        puts.append(put)
-    for put in puts + [put_cost]:
+    for put in puts:
         put.wait()
 
 
@@ -491,16 +493,17 @@
     dma = pltpu.SemaphoreType.DMA
     f32, i32, bf16 = jnp.float32, jnp.int32, jnp.bfloat16
     args = (points, centroids, assign.reshape(1, ROWS), keep_mask.reshape(1, ROWS))
-    words, steps, cost = pl.pallas_call(
+    rows, cost = pl.pallas_call(
         update_kernel,
         out_shape=(
-            jax.ShapeDtypeStruct((2, N, N, NZ, PAIRS, LANES), i32),
-            jax.ShapeDtypeStruct((2, N, N, NZ, 1, LANES), f32),
+            jax.ShapeDtypeStruct((2048, 1024), f32),
             jax.ShapeDtypeStruct((1, ROWS), f32),
         ),
         in_specs=[hbm] * 4,
-        out_specs=(vmem, vmem, vmem),
+        out_specs=(vmem, vmem),
         scratch_shapes=[
+            pltpu.VMEM((2, N, N, NZ, PAIRS, LANES), i32),
+            pltpu.VMEM((2, N, N, NZ, 1, LANES), f32),
             pltpu.VMEM((ROWS, 1024), bf16),
             pltpu.VMEM((2, 2048, 1024), bf16),
             pltpu.VMEM((2, 1, ROWS), i32),
@@ -527,14 +530,14 @@
         ),
     )(*(pltpu.with_memory_space_constraint(a, pltpu.HBM) for a in args))
     new_centroids, cost = pl.pallas_call(
-        decode_kernel,
+        put_kernel,
         out_shape=(jax.ShapeDtypeStruct((2048, 1024), f32), jax.ShapeDtypeStruct((1, ROWS), f32)),
-        in_specs=[vmem] * 3,
+        in_specs=[vmem] * 2,
         out_specs=(hbm, hbm),
-        scratch_shapes=[pltpu.VMEM((N, CROWS, 1024), f32), dma((N + 1,))],
-        compiler_params=pltpu.CompilerParams(vmem_limit_bytes=12 * 1024 * 1024),
-        cost_estimate=pl.CostEstimate(flops=8 << 20, bytes_accessed=12 << 20, transcendentals=0),
-    )(words, steps, cost)
+        scratch_shapes=[dma((N + 1,))],
+        compiler_params=pltpu.CompilerParams(vmem_limit_bytes=1024 * 1024),
+        cost_estimate=pl.CostEstimate(flops=0, bytes_accessed=16 << 20, transcendentals=0),
+    )(rows, cost)
     return new_centroids, cost.reshape(ROWS)
 
 

time: 84.6 us -> 78 us (0.922); the launches traced: 84.3 us -> 76.5 us
  Pallas kernels: 83.7 us -> 75.9 us
    pallas_call x2, Pallas kernels: 83.7 us -> 75.9 us  [the longest x1 72.5 us: shards(): pl.pallas_call(update_kernel, out_shape=(jax.ShapeDtypeStruct((2048, 1024...]
where the time goes in v3:
time: 78 us; the launch traced here: 76.5 us
  Pallas kernels  75.9 us (97%)
    pallas_call x1, Pallas kernels, shards(): pl.pallas_call(update_kernel, out_shape=(jax.ShapeDtypeStruct((2048, 1024...  72.5 us
    pallas_call x1, Pallas kernels, shards(): pl.pallas_call(put_kernel, out_shape=(jax.ShapeDtypeStruct((2048, 1024),...  3.38 us

profile of v3, /device:TPU:2, one launch (start us, length us, event | category | flops | bytes accessed | tf_op | source)
XLA Modules:
  0.0 76.5 jit_solution(5196043503902222438)
XLA Ops:
  0.6 72.5 %shard_map.59 = (f32[2048,1024]{1,0:T(8,128)S(1)}, f32[1,512]{1,0:T(1,128)S(1)}) custom-call(bf16[512,1024]{1,0:T(8,128)(2,1)} %p_hbm.1, bf16[2048,1024]{1,0:T(8,128)(2,1)} %c_hbm.1, s32[1,512]{1,0:T(1,128)} %bitcast.3, s32[1,512]{1,0:T(1,128)} %bitcast.4), custom_call_target="tpu_custom_call" | custom-call | tf_op jit(solution)/shard_map/pallas_call | solution.py:496
  73.1 3.4 %shard_map.60 = (f32[2048,1024]{1,0:T(8,128)}, f32[1,512]{1,0:T(1,128)}) custom-call(f32[2048,1024]{1,0:T(8,128)S(1)} %get-tuple-element.6.rows_ref, f32[1,512]{1,0:T(1,128)S(1)} %get-tuple-element.7.cost_ref), custom_call_target="tpu_custom_call" | custom-call | bytes 16777216 | tf_op jit(solution)/shard_map/pallas_call | solution.py:532

commit v4 on v3

--- a/solution.py
+++ b/solution.py
@@ -169,13 +169,14 @@
     def hits(id_row, base):
         local = id_row - base
         local = jnp.where((local >= 0) & (local < TILE), local, -1).astype(jnp.float32)
-        local = jnp.broadcast_to(local, (16, 2 * ROWS)).astype(jnp.bfloat16)
+        width = id_row.shape[1]
+        local = jnp.broadcast_to(local, (16, width)).astype(jnp.bfloat16)
         at = lax.broadcasted_iota(jnp.int32, (TILE, LANES), 0).astype(jnp.float32).astype(jnp.bfloat16)
         at = at.reshape(TILE // 16, 16, LANES)
         one, zero = jnp.ones((), jnp.bfloat16), jnp.zeros((), jnp.bfloat16)
         parts = [
             jnp.where(at == local[None, :, i * LANES : (i + 1) * LANES], one, zero).reshape(TILE, LANES)
-            for i in range(2 * ROWS // LANES)
+            for i in range(width // LANES)
         ]
         count = parts[0]
         for part in parts[1:]:
@@ -187,15 +188,15 @@
         high, count_high = hits(id_row, base + TILE)
         return jnp.concatenate([low, high], axis=0), jnp.concatenate([count_low, count_high], axis=0)
 
-    def accumulate(c, two, q):
-        where = pl.ds((two - 1) * 2 * ROWS, 2 * ROWS)
-        hit, count = hits_chunk(ids[c, :, where], m * 2048 + q * CROWS)
+    def accumulate(c, first, count, q):
+        where = pl.ds((first - 2) * ROWS, count * ROWS)
+        hit, number = hits_chunk(ids[c, :, where], m * 2048 + q * CROWS)
         acc[c, q] += jnp.dot(hit, near[c, where, :], preferred_element_type=jnp.float32)
-        cnt[c, q] += count
-
-    def accumulate_all(c, two):
+        cnt[c, q] += number
+
+    def accumulate_all(c, first, count):
         def body(q, carry):
-            accumulate(c, two, q)
+            accumulate(c, first, count, q)
             return carry
 
         lax.fori_loop(0, N, body, 0)
@@ -242,22 +243,20 @@
         arrive(k.from_r)
         k.two += to_partner(k, 3, 5)
     phase("acc1")
-    accumulate_all(0, 1)
+    accumulate_all(0, 2, 2)
     phase("w_o")
     for k in colours:
         arrive(k.from_o)
         k.three = to_partner(k, 6, 7)
-    phase("acc1b")
-    accumulate_all(1, 1)
     phase("w_plr")
     for k in colours:
         arrive(k.two)
     phase("acc2")
-    for k in colours:
-        accumulate_all(k.c, 2)
+    accumulate_all(1, 2, 4)
     phase("w_po")
     for k in colours:
         arrive(k.three)
+    colours[0].rest, colours[1].rest = (4, 4), (6, 2)
 
     def pack(c, q, words, aux):
         def block(b, carry):
@@ -277,7 +276,7 @@
             yaux[k.c, s, b, 0:1, :] = step
             yaux[k.c, s, b, 1:2, :] = count
 
-        accumulate(k.c, 3, q)
+        accumulate(k.c, *k.rest, q)
         pack(k.c, q, lambda zb: ysend.at[k.c, s, zb], aux)
 
     h0, h1 = pl.ds(0, NZ // 2), pl.ds(NZ // 2, NZ // 2)
@@ -305,7 +304,7 @@
         k.yrelay_r.wait_recv()
         k.y_o.append(remote(yrecv.at[k.c, 3, h1], yrecv.at[k.c, 2, h1], k.at_r(k.rl)))
     for k in colours:
-        accumulate(k.c, 3, k.r)
+        accumulate(k.c, *k.rest, k.r)
 
     def unpack(k, s):
         def block(b, carry):
@@ -375,97 +374,158 @@
         prior = cv[0, rows, k.cols(k.f)].astype(jnp.float32)
         sums = jnp.concatenate([k.high, k.low], axis=0)
         code, step = encode(jnp.where(count > 0.5, sums / jnp.maximum(count, 1.0), prior))
-        words_ref[k.c, k.f, k.r, z] = pair(code)
-        steps_ref[k.c, k.f, k.r, z] = to_row(step, lane_eye(OWN))
-        k.start = []
-        for to in (k.ro, k.rr, k.rl):
-            for ref in (steps_ref, words_ref):
-                own_piece = ref.at[k.c, k.f, k.r, z]
-                k.start.append(remote(own_piece, own_piece, k.at_r(to)))
-
-    def group(k, f, zc, device):
-        copies = []
-        for ref in (steps_ref, words_ref):
-            piece = ref.at[k.c, f, :, zc]
+        words_ref[k.c, k.f, 0, z] = pair(code)
+        steps_ref[k.c, k.f, 0, z] = to_row(step, lane_eye(OWN))
+
+    parts = (pl.ds(0, 1), pl.ds(1, N - 1))
+
+    def hop(k, way, h, s):
+        zc, device = zat(-way * (h - 1)), at_z(zat(way))
+        piece = words_ref.at[k.c, k.f, s, zc]
+        copies = [remote(piece, piece, device)]
+        if s == 2:
+            piece = steps_ref.at[k.c, k.f, :, zc]
+            copies.append(remote(piece, piece, device))
+        k.hops[way, h, s] = copies
+
+    def group(k, f, zc, part, device):
+        piece = words_ref.at[k.c, f, parts[part], zc]
+        copies = [remote(piece, piece, device)]
+        if part:
+            piece = steps_ref.at[k.c, f, :, zc]
             copies.append(remote(piece, piece, device))
         return copies
 
-    def hop(k, way, h, half):
-        zc, device = zat(-way * (h - 1)), at_z(zat(way))
-        copies = []
-        if half == 0:
-            piece = steps_ref.at[k.c, k.f, :, zc]
-            copies.append(remote(piece, piece, device))
-        piece = words_ref.at[k.c, k.f, pl.ds(half * (N // 2), N // 2), zc]
-        copies.append(remote(piece, piece, device))
-        k.hops[way, h, half] = copies
-
-    def spread(k, d):
+    def spread(k, d, part):
         zc = zat(d)
-        k.side[d] = (group(k, k.f, zc, k.at_f(k.fr)), group(k, k.f, zc, k.at_f(k.fl)))
+        k.side[d, part] = (group(k, k.f, zc, part, k.at_f(k.fr)), group(k, k.f, zc, part, k.at_f(k.fl)))
+        if d in (-3, 3, 4):
+            k.far[d, part] = group(k, k.f, zc, part, k.at_f(k.fo))
 
     def left_first(d):
         return d in (0, 1, 2, 3)
 
-    def across(k, d):
+    def across(k, d, part):
         zc = zat(d)
-        from_left, from_right = k.side[d]
+        from_left, from_right = k.side[d, part]
         if left_first(d):
             arrive(from_left)
-            k.last[d] = (group(k, k.fl, zc, k.at_f(k.fr)), from_right)
+            k.last[d, part] = group(k, k.fl, zc, part, k.at_f(k.fr)) + from_right
         else:
             arrive(from_right)
-            k.last[d] = (group(k, k.fr, zc, k.at_f(k.fl)), from_left)
+            k.last[d, part] = group(k, k.fr, zc, part, k.at_f(k.fl)) + from_left
 
     def finish(groups):
-        def block(r, carry):
+        def block(s, carry):
             for k, f, d in groups:
                 zc = zat(d)
-                step = to_col(steps_ref[k.c, f, r, zc], lane_eye(OWN))
-                high, low = decode(words_ref[k.c, f, r, zc], step)
-                base = pl.multiple_of((r * NZ + zc) * OWN, OWN)
+                step = to_col(steps_ref[k.c, f, s, zc], lane_eye(OWN))
+                high, low = decode(words_ref[k.c, f, s, zc], step)
+                base = pl.multiple_of((lax.rem(k.r + s, N) * NZ + zc) * OWN, OWN)
                 out_ref[pl.ds(base, PAIRS), k.cols(f)] = high
                 out_ref[pl.ds(base + PAIRS, PAIRS), k.cols(f)] = low
             return carry
 
         lax.fori_loop(0, N, block, 0)
 
-    phase("g1")
-    for k in colours:
-        arrive(k.start)
-        k.hops, k.side, k.last = {}, {}, {}
-        for half in (0, 1):
-            for way in (1, -1):
-                hop(k, way, 1, half)
-        spread(k, 0)
-    rounds = ((0,), (-1, 1), (-2, 2), (-3, 3), (4,))
-    for h in range(1, 7):
-        if h <= 4:
-            phase(f"g_z{h}")
-            for k in colours:
-                for half in (0, 1):
-                    for way in (1, -1):
-                        if h < 4 or way == (1, -1)[half]:
-                            arrive(k.hops[way, h, half])
-                            if h < 3 or (h == 3 and way == (1, -1)[half]):
-                                hop(k, way, h + 1, half)
-                for d in rounds[h]:
-                    spread(k, d)
-        if h <= 5:
-            phase(f"g_x{h}")
-            for k in colours:
-                for d in rounds[h - 1]:
-                    across(k, d)
-        phase(f"g_f{h}")
-        groups = []
+    def own_done(*ds):
+        return [(k, k.f, d) for k in colours for d in ds]
+
+    def first_done(*ds):
+        return [(k, k.fl if left_first(d) else k.fr, d) for k in colours for d in ds]
+
+    def last_done(*ds):
         for k in colours:
-            for d in rounds[h - 1] if h <= 5 else ():
-                groups += [(k, k.f, d), (k, k.fl if left_first(d) else k.fr, d)]
-            for d in rounds[h - 2] if h >= 2 else ():
-                for copies in k.last[d]:
-                    arrive(copies)
-                groups += [(k, k.fo, d), (k, k.fr if left_first(d) else k.fl, d)]
-        finish(groups)
+            for d in ds:
+                arrive(k.last[d, 0] + k.last[d, 1])
+        return [(k, f, d) for k in colours for d in ds for f in (k.fo, k.fr if left_first(d) else k.fl)]
+
+    def far_way(k, s):
+        return 1 if (s < 2) == (k.c == 0) else -1
+
+    def z_round(h, chunks, part):
+        phase(f"g_z{h}p{part}")
+        for k in colours:
+            for s in chunks:
+                for way in (1, -1):
+                    if h < 4 or way == far_way(k, s):
+                        arrive(k.hops[way, h, s])
+                        if h < 3 or (h == 3 and way == far_way(k, s)):
+                            hop(k, way, h + 1, s)
+            for d in ((-h, h) if h < 4 else (4,)):
+                spread(k, d, part)
+
+    def x_round(part, *ds):
+        phase("g_x%d" % part)
+        for k in colours:
+            for d in ds:
+                across(k, d, part)
+
+    def hop_opposite(way, h):
+        zc, device = zat(-way * (h - 1)), at_z(zat(way))
+        for k in colours:
+            k.opposite[way, h] = group(k, k.fo, zc, 0, device) + group(k, k.fo, zc, 1, device)
+
+    def opposite_done(h):
+        for k in colours:
+            arrive(k.opposite[1, h] + k.opposite[-1, h])
+        return [(k, k.fo, d) for k in colours for d in (-h, h)]
+
+    def sides_done(*ds):
+        for k in colours:
+            for d in ds:
+                for part in (0, 1):
+                    arrive(k.side[d, part][0] + k.side[d, part][1])
+        return [(k, f, d) for k in colours for d in ds for f in (k.fl, k.fr)]
+
+    phase("g_0")
+    for k in colours:
+        k.hops, k.side, k.last, k.start, k.opposite, k.far = {}, {}, {}, {}, {}, {}
+        for s, to in ((2, k.ro), (3, k.rr), (1, k.rl)):
+            k.start[s] = [
+                remote(ref.at[k.c, k.f, 0, z], ref.at[k.c, k.f, s, z], k.at_r(to)) for ref in (words_ref, steps_ref)
+            ]
+        hop(k, 1, 1, 0)
+        hop(k, -1, 1, 0)
+        spread(k, 0, 0)
+    z_round(1, (0,), 0)
+    phase("g_1")
+    for k in colours:
+        for s in (3, 1, 2):
+            arrive(k.start[s])
+            hop(k, 1, 1, s)
+            hop(k, -1, 1, s)
+        spread(k, 0, 1)
+    x_round(0, 0)
+    z_round(2, (0,), 0)
+    z_round(1, (3, 1, 2), 1)
+    x_round(1, 0)
+    z_round(3, (0,), 0)
+    phase("g_f1")
+    finish(own_done(0, -1, 1) + first_done(0))
+    z_round(2, (3, 1, 2), 1)
+    phase("g_o1")
+    done = last_done(0)
+    hop_opposite(1, 1)
+    hop_opposite(-1, 1)
+    z_round(4, (0,), 0)
+    x_round(0, -2, 2)
+    phase("g_f2")
+    finish(own_done(-2, 2) + done + sides_done(-1, 1))
+    z_round(3, (3, 1, 2), 1)
+    x_round(1, -2, 2)
+    phase("g_f3")
+    finish(own_done(-3, 3) + first_done(-2, 2))
+    z_round(4, (3, 1, 2), 1)
+    phase("g_f4")
+    finish(own_done(4) + opposite_done(1) + last_done(-2, 2))
+    phase("g_f5")
+    finish(sides_done(-3, 3))
+    phase("g_f6")
+    for k in colours:
+        for d in (-3, 3, 4):
+            arrive(k.far[d, 0] + k.far[d, 1])
+    finish([(k, k.fo, d) for k in colours for d in (-3, 3, 4)] + sides_done(4))
     phase("w_send")
     for copy in used:
         copy.wait_send()
@@ -473,7 +533,7 @@
     assert len(used) == N_COPIES, len(used)
 
 
-N_COPIES = 216
+N_COPIES = 292
 
 
 def put_kernel(rows_ref, cost_ref, rows_hbm, cost_hbm, sems):

time: 78 us -> 75.4 us (0.967); the launches traced: 76.5 us -> 75.3 us
  Pallas kernels: 75.9 us -> 74.7 us
    pallas_call x1, Pallas kernels: 72.5 us -> 71.3 us  [shards(): pl.pallas_call(update_kernel, out_shape=(jax.ShapeDtypeStruct((2048, 1024...]
where the time goes in v4:
time: 75.4 us; the launch traced here: 75.3 us
  Pallas kernels  74.7 us (99%)
    pallas_call x1, Pallas kernels, shards(): pl.pallas_call(update_kernel, out_shape=(jax.ShapeDtypeStruct((2048, 1024...  71.3 us
    pallas_call x1, Pallas kernels, shards(): pl.pallas_call(put_kernel, out_shape=(jax.ShapeDtypeStruct((2048, 1024),...  3.38 us

profile of v4, /device:TPU:2, one launch (start us, length us, event | category | flops | bytes accessed | tf_op | source)
XLA Modules:
  0.0 75.3 jit_solution(8618006626694933907)
XLA Ops:
  0.6 71.3 %shard_map.59 = (f32[2048,1024]{1,0:T(8,128)S(1)}, f32[1,512]{1,0:T(1,128)S(1)}) custom-call(bf16[512,1024]{1,0:T(8,128)(2,1)} %p_hbm.1, bf16[2048,1024]{1,0:T(8,128)(2,1)} %c_hbm.1, s32[1,512]{1,0:T(1,128)} %bitcast.3, s32[1,512]{1,0:T(1,128)} %bitcast.4), custom_call_target="tpu_custom_call" | custom-call | tf_op jit(solution)/shard_map/pallas_call | solution.py:556
  71.9 3.4 %shard_map.60 = (f32[2048,1024]{1,0:T(8,128)}, f32[1,512]{1,0:T(1,128)}) custom-call(f32[2048,1024]{1,0:T(8,128)S(1)} %get-tuple-element.6.rows_ref, f32[1,512]{1,0:T(1,128)S(1)} %get-tuple-element.7.cost_ref), custom_call_target="tpu_custom_call" | custom-call | bytes 16777216 | tf_op jit(solution)/shard_map/pallas_call | solution.py:592

commit v5 on v3

v5 whole, which is shorter than its diff:
```python
import jax
import jax.numpy as jnp
from jax import lax
from jax.experimental import pallas as pl
from jax.experimental.pallas import tpu as pltpu
from jax.sharding import Mesh
from jax.sharding import PartitionSpec as P

STEPS = 32000.0
TINY = 2.0**-100
N, NZ = 4, 8
LANES = 128
CROWS = 512
HROWS = CROWS // 2
OWN = HROWS // NZ
PAIRS = OWN // 2
TILE = 256
ROWS = 512
MESH_ID = pl.DeviceIdType.MESH


def encode(v):
    top = jnp.maximum(jnp.max(jnp.abs(v), axis=1, keepdims=True), TINY)
    code = jnp.floor(v * (STEPS / top) + 0.5).astype(jnp.int32)
    return code, top * (1.0 / STEPS)


def pair(code):
    return (code[:PAIRS] << 16) | (code[PAIRS:] & 0xFFFF)


def decode(words, step):
    high = (words >> 16).astype(jnp.float32)
    low = ((words << 16) >> 16).astype(jnp.float32)
    return high * step[:PAIRS], low * step[PAIRS:]


def lane_eye(rows, shift=0):
    at_row = lax.broadcasted_iota(jnp.int32, (rows, LANES), 0)
    at_lane = lax.broadcasted_iota(jnp.int32, (rows, LANES), 1)
    return at_lane == at_row + shift


def to_row(col, eye):
    return jnp.sum(jnp.where(eye, col, 0.0), axis=0, keepdims=True)


def to_col(row, eye):
    return jnp.sum(jnp.where(eye, row, 0.0), axis=1, keepdims=True)


def update_kernel(
    p_hbm, c_hbm, assign_hbm, keep_hbm, out_ref, cost_ref,
    words_ref, steps_ref,
    pv, cv, idv, near0, near, ids0, ids, relay, best, acc, cnt,
    ysend, yaux, yrecv, yauxr, zsend, zaux, zrecv, zauxr,
    send_sem, recv_sem, local_sem,
):
    z, y, x, m = (lax.axis_index(n) for n in ("z", "y", "x", "mp"))
    zat = lambda d: lax.rem(z + d + NZ, NZ)
    used = []
    scopes = []

    def phase(name):
        if scopes:
            scopes.pop().__exit__(None, None, None)
        if name:
            scopes.append(jax.named_scope(name))
            scopes[-1].__enter__()

    def remote(src, dst, device):
        k = len(used)
        copy = pltpu.make_async_remote_copy(
            src_ref=src, dst_ref=dst, send_sem=send_sem.at[k], recv_sem=recv_sem.at[k],
            device_id=device, device_id_type=MESH_ID,
        )
        copy.start()
        used.append(copy)
        return copy

    def arrive(copies):
        for copy in copies:
            copy.wait_recv()

    at_x = lambda to: (z, y, to, m)
    at_y = lambda to: (z, to, x, m)
    at_z = lambda to: (to, y, x, m)
    partner = (z, y, x, 1 - m)

    class Colour:
        def __init__(self, c, first, second, at_first, at_second, at_second_z):
            self.c, self.f, self.r = c, first, second
            self.fr, self.fl, self.fo = (lax.rem(first + d, N) for d in (1, 3, 2))
            self.rr, self.rl, self.ro = (lax.rem(second + d, N) for d in (1, 3, 2))
            self.at_f, self.at_r, self.at_rz = at_first, at_second, at_second_z

        def cols(self, f):
            return pl.ds(pl.multiple_of(self.c * 512 + f * LANES, LANES), LANES)

    at_xz = lambda to, to_z: (to_z, y, to, m)
    at_yz = lambda to, to_z: (to_z, to, x, m)
    colours = (Colour(0, x, y, at_x, at_y, at_yz), Colour(1, y, x, at_y, at_x, at_xz))

    phase("enter")
    loads = [
        pltpu.make_async_copy(p_hbm, pv, local_sem.at[0]),
        pltpu.make_async_copy(assign_hbm, idv.at[0], local_sem.at[1]),
        pltpu.make_async_copy(keep_hbm, idv.at[1], local_sem.at[2]),
    ]
    load_c = pltpu.make_async_copy(c_hbm, cv.at[0], local_sem.at[3])
    for copy in loads + [load_c]:
        copy.start()

    peers = [partner] + [at_z(zat(d)) for d in range(1, NZ)]
    for k in colours:
        peers += [k.at_f(k.fr), k.at_f(k.fl), k.at_f(k.fo)]
        peers += [k.at_rz(to, zat(d)) for to in (k.rr, k.rl, k.ro) for d in (1, -1)]
    barrier = pltpu.get_barrier_semaphore()
    for peer in peers:
        pl.semaphore_signal(barrier, inc=1, device_id=peer, device_id_type=MESH_ID)
    for copy in loads:
        copy.wait()
    ids0[:, :ROWS] = jnp.where(idv[1] > 0, idv[0], -1)
    best[...] = jnp.full(best.shape, jnp.inf, jnp.float32)
    pl.semaphore_wait(barrier, len(peers))

    phase("send_p")

    def slot(s):
        return pl.ds((s - 2) * ROWS, ROWS)

    lo, hi = pl.ds(0, ROWS // 2), pl.ds(ROWS // 2, ROWS // 2)
    mine_ids = ids0.at[:, pl.ds(0, ROWS)]
    for k in colours:
        k.relay_l = remote(pv.at[lo, k.cols(k.fo)], relay.at[k.c, 0], k.at_f(k.fr))
        k.relay_r = remote(pv.at[hi, k.cols(k.fo)], relay.at[k.c, 1], k.at_f(k.fl))
    own = []
    from_p = [remote(mine_ids, ids0.at[:, pl.ds(ROWS, ROWS)], partner)]
    for k in colours:
        lanes = pl.ds(k.c * LANES, LANES)
        own.append(
            pltpu.make_async_copy(pv.at[:, k.cols(k.f)], near0.at[pl.ds(0, ROWS), lanes], local_sem.at[4 + k.c])
        )
        own[-1].start()
        from_p.append(remote(pv.at[:, k.cols(k.f)], near0.at[pl.ds(ROWS, ROWS), lanes], partner))
    for k in colours:
        k.from_l = [
            remote(mine_ids, ids.at[k.c, :, slot(2)], k.at_f(k.fr)),
            remote(pv.at[:, k.cols(k.fr)], near.at[k.c, slot(2)], k.at_f(k.fr)),
        ]
        k.from_r = [
            remote(mine_ids, ids.at[k.c, :, slot(3)], k.at_f(k.fl)),
            remote(pv.at[:, k.cols(k.fl)], near.at[k.c, slot(3)], k.at_f(k.fl)),
        ]
        k.from_o = [remote(mine_ids, ids.at[k.c, :, slot(6)], k.at_f(k.fo))]
    c_p = remote(c_hbm, cv.at[1], partner)

    def distances(s, first, count):
        def tile(t, carry):
            part = cv[s, pl.ds(pl.multiple_of(t * TILE, TILE), TILE), :]
            inner = lax.dot_general(
                part, pv[...], (((1,), (1,)), ((), ())), preferred_element_type=jnp.float32
            )
            wide = part.astype(jnp.float32)
            square = jnp.sum(wide * wide, axis=1, keepdims=True)
            dist = square - 2.0 * inner
            low = jnp.min(dist.reshape(TILE // 8, 8, ROWS), axis=0)
            best[...] = jnp.minimum(best[...], low)
            return carry

        lax.fori_loop(first, first + count, tile, 0)

    def hits(id_row, base):
        local = id_row - base
        local = jnp.where((local >= 0) & (local < TILE), local, -1).astype(jnp.float32)
        width = id_row.shape[1]
        local = jnp.broadcast_to(local, (16, width)).astype(jnp.bfloat16)
        at = lax.broadcasted_iota(jnp.int32, (TILE, LANES), 0).astype(jnp.float32).astype(jnp.bfloat16)
        at = at.reshape(TILE // 16, 16, LANES)
        one, zero = jnp.ones((), jnp.bfloat16), jnp.zeros((), jnp.bfloat16)
        parts = [
            jnp.where(at == local[None, :, i * LANES : (i + 1) * LANES], one, zero).reshape(TILE, LANES)
            for i in range(width // LANES)
        ]
        count = parts[0]
        for part in parts[1:]:
            count = count + part
        return jnp.concatenate(parts, axis=1), count

    def hits_chunk(id_row, base):
        low, count_low = hits(id_row, base)
        high, count_high = hits(id_row, base + TILE)
        return jnp.concatenate([low, high], axis=0), jnp.concatenate([count_low, count_high], axis=0)

    def accumulate(c, first, count, q):
        where = pl.ds((first - 2) * ROWS, count * ROWS)
        hit, number = hits_chunk(ids[c, :, where], m * 2048 + q * CROWS)
        part = jnp.dot(hit, near[c, where, :], preferred_element_type=jnp.float32)
        acc[c, q] += part.reshape(2, HROWS, LANES)
        cnt[c, q] += number.reshape(2, HROWS, LANES)

    def accumulate_others(k, first, count):
        def body(j, carry):
            accumulate(k.c, first, count, lax.rem(k.r + 1 + j, N))
            return carry

        lax.fori_loop(0, N - 1, body, 0)

    def accumulate_own():
        def body(q, carry):
            hit, count = hits_chunk(ids0[...], m * 2048 + q * CROWS)
            part = jnp.dot(hit, near0[...], preferred_element_type=jnp.float32)
            for c in range(2):
                acc[c, q] = part[:, c * LANES : (c + 1) * LANES].reshape(2, HROWS, LANES)
                cnt[c, q] = count.reshape(2, HROWS, LANES)
            return carry

        lax.fori_loop(0, N, body, 0)

    phase("dist0a")
    load_c.wait()
    distances(0, 0, 4)
    phase("w_own")
    for copy in own:
        copy.wait()
    arrive(from_p)
    phase("acc0")
    accumulate_own()
    phase("w_relay")
    for k in colours:
        k.relay_l.wait_recv()
        k.from_o.append(remote(relay.at[k.c, 0], near.at[k.c, pl.ds(4 * ROWS, ROWS // 2)], k.at_f(k.fr)))
        k.relay_r.wait_recv()
        k.from_o.append(remote(relay.at[k.c, 1], near.at[k.c, pl.ds(4 * ROWS + ROWS // 2, ROWS // 2)], k.at_f(k.fl)))
    phase("dist0b")
    distances(0, 4, 4)

    def to_partner(k, source, target):
        return [
            remote(near.at[k.c, slot(source)], near.at[k.c, slot(target)], partner),
            remote(ids.at[k.c, :, slot(source)], ids.at[k.c, :, slot(target)], partner),
        ]

    phase("w_lr")
    for k in colours:
        arrive(k.from_l)
        k.two = to_partner(k, 2, 4)
        arrive(k.from_r)
        k.two += to_partner(k, 3, 5)
    phase("acc1")
    accumulate_others(colours[0], 2, 2)
    phase("w_o")
    for k in colours:
        arrive(k.from_o)
        k.three = to_partner(k, 6, 7)
    phase("w_plr")
    for k in colours:
        arrive(k.two)
    phase("acc2")
    accumulate_others(colours[1], 2, 4)
    phase("w_po")
    for k in colours:
        arrive(k.three)
    colours[0].rest, colours[1].rest = (4, 4), (6, 2)

    def pack(c, q, h, words, aux):
        for b in range(HROWS // LANES):
            eye = lane_eye(LANES)
            rows = pl.ds(b * LANES, LANES)
            code, step = encode(acc[c, q, h, rows, :])
            for j in range(LANES // OWN):
                words(b * (LANES // OWN) + j)[...] = pair(code[j * OWN : (j + 1) * OWN])
            count = jnp.sum(cnt[c, q, h, rows, :].astype(jnp.float32), axis=1, keepdims=True)
            aux(b, to_row(step, eye), to_row(count, eye))

    def send_sums(k, s, q, h):
        def aux(b, step, count):
            yaux[k.c, s, h, b, 0:1, :] = step
            yaux[k.c, s, h, b, 1:2, :] = count

        pack(k.c, q, h, lambda zb: ysend.at[k.c, s, h, zb], aux)
        k.sums[s, h] = [
            remote(ysend.at[k.c, s, h], yrecv.at[k.c, s, h], k.at_r(q)),
            remote(yaux.at[k.c, s, h], yauxr.at[k.c, s, h], k.at_r(q)),
        ]

    phase("y_pack")
    order = [(k, 2, k.ro) for k in colours] + [(k, s, q) for k in colours for s, q in ((0, k.rr), (1, k.rl))]
    for k in colours:
        k.sums = {}
    for k, s, q in order:
        accumulate(k.c, *k.rest, q)
        send_sums(k, s, q, 0)
    phase("y_packq")
    for k, s, q in order:
        send_sums(k, s, q, 1)
    phase("y_own")
    for k in colours:
        accumulate(k.c, 2, 6, k.r)

    def unpack(k, s, h):
        for b in range(HROWS // LANES):
            step = to_col(yauxr[k.c, s, h, b, 0:1, :], lane_eye(LANES))
            for j in range(LANES // OWN):
                high, low = decode(yrecv[k.c, s, h, b * (LANES // OWN) + j], step[j * OWN : (j + 1) * OWN])
                base = b * LANES + j * OWN
                acc[k.c, k.r, h, pl.ds(base, PAIRS), :] += high
                acc[k.c, k.r, h, pl.ds(base + PAIRS, PAIRS), :] += low

    zcopies = {}

    def z_send(h):
        phase(f"y_unpack{h}")
        for s in (0, 1, 2):
            for k in colours:
                arrive(k.sums[s, h])
                unpack(k, s, h)
        phase(f"z_pack{h}")
        for k in colours:
            def aux(b, step, count, k=k):
                zaux[h, b, 2 * k.c : 2 * k.c + 1, :] = step
                for s in range(3):
                    count = count + yauxr[k.c, s, h, b, 1:2, :]
                zaux[h, b, 2 * k.c + 1 : 2 * k.c + 2, :] = count

            pack(k.c, k.r, h, lambda zb, k=k: zsend.at[h, zb, k.c], aux)
        for d in (4, 3, 5, 2, 6, 1, 7):
            to = zat(d)
            zcopies[h, d] = [
                remote(zaux.at[h, to // (LANES // OWN)], zauxr.at[h, d - 1], at_z(to)),
                remote(zsend.at[h, to], zrecv.at[h, d - 1], at_z(to)),
            ]

    def own_to_slot(h, k, s, device):
        return [
            remote(ref.at[h, k.c, k.f, 0, z], ref.at[h, k.c, k.f, s, z], device) for ref in (words_ref, steps_ref)
        ]

    def z_sum(h):
        phase(f"z_sum{h}")
        mine = lane_eye(OWN, lax.rem(z, LANES // OWN) * OWN)
        for k in colours:
            sums = acc[k.c, k.r, h, pl.ds(pl.multiple_of(z * OWN, OWN), OWN), :]
            k.high, k.low = sums[:PAIRS], sums[PAIRS:]
            k.count = zaux[h, z // (LANES // OWN), 2 * k.c + 1 : 2 * k.c + 2, :]
        for d in (1, 7, 2, 6, 3, 5, 4):
            arrive(zcopies[h, d])
            for k in colours:
                step = to_col(zauxr[h, d - 1, 2 * k.c : 2 * k.c + 1, :], mine)
                high, low = decode(zrecv[h, d - 1, k.c], step)
                k.high, k.low = k.high + high, k.low + low
                k.count = k.count + zauxr[h, d - 1, 2 * k.c + 1 : 2 * k.c + 2, :]
        phase(f"fresh{h}")
        for k in colours:
            count = to_col(k.count, mine)
            rows = pl.ds(pl.multiple_of(k.r * CROWS + h * HROWS + z * OWN, OWN), OWN)
            prior = cv[0, rows, k.cols(k.f)].astype(jnp.float32)
            sums = jnp.concatenate([k.high, k.low], axis=0)
            code, step = encode(jnp.where(count > 0.5, sums / jnp.maximum(count, 1.0), prior))
            words_ref[h, k.c, k.f, 0, z] = pair(code)
            steps_ref[h, k.c, k.f, 0, z] = to_row(step, lane_eye(OWN))
            to_slots = ((2, k.ro), (3, k.rr), (1, k.rl))
            k.start[h] = sum((own_to_slot(h, k, s, k.at_r(to)) for s, to in to_slots), [])
        for k in colours if h == 0 else ():
            for way in (1, -1):
                to_slots = ((2, k.ro), (3, k.rr), (1, k.rl), (0, k.r))
                k.hops[h, way, 1] = sum((own_to_slot(h, k, s, k.at_rz(to, zat(way))) for s, to in to_slots), [])

    def group(h, k, f, zc, device):
        copies = []
        for ref in (words_ref, steps_ref):
            piece = ref.at[h, k.c, f, :, zc]
            copies.append(remote(piece, piece, device))
        return copies

    def hop(h, k, way, n):
        k.hops[h, way, n] = group(h, k, k.f, zat(-way * (n - 1)), at_z(zat(way)))

    def spread(h, k, d):
        targets = (k.fr, k.fl, k.fo) if (h, d) in STRAIGHT else (k.fr, k.fl)
        k.side[h, d] = [group(h, k, k.f, zat(d), k.at_f(to)) for to in targets]

    def left_first(d):
        return d in (0, 1, 2, 3)

    def across(h, *ds):
        phase(f"g_x{h}")
        for d in ds:
            for k in colours:
                from_left, from_right = k.side[h, d]
                if left_first(d):
                    arrive(from_left)
                    k.last[h, d] = group(h, k, k.fl, zat(d), k.at_f(k.fr)) + from_right
                else:
                    arrive(from_right)
                    k.last[h, d] = group(h, k, k.fr, zat(d), k.at_f(k.fl)) + from_left

    def finish(groups):
        def block(s, carry):
            for h, k, f, d in groups:
                zc = zat(d)
                step = to_col(steps_ref[h, k.c, f, s, zc], lane_eye(OWN))
                high, low = decode(words_ref[h, k.c, f, s, zc], step)
                base = pl.multiple_of(lax.rem(k.r + s, N) * CROWS + h * HROWS + zc * OWN, OWN)
                out_ref[pl.ds(base, PAIRS), k.cols(f)] = high
                out_ref[pl.ds(base + PAIRS, PAIRS), k.cols(f)] = low
            return carry

        lax.fori_loop(0, N, block, 0)

    def own_done(h, *ds):
        return [(h, k, k.f, d) for k in colours for d in ds]

    def first_done(h, *ds):
        return [(h, k, k.fl if left_first(d) else k.fr, d) for k in colours for d in ds]

    def last_done(h, *ds):
        groups = []
        for k in colours:
            for d in ds:
                if (h, d) in STRAIGHT:
                    arrive(sum(k.side[h, d], []))
                    groups += [(h, k, f, d) for f in (k.fl, k.fr, k.fo)]
                else:
                    arrive(k.last[h, d])
                    groups += [(h, k, f, d) for f in (k.fo, k.fr if left_first(d) else k.fl)]
        return groups

    def sides_done(h, *ds):
        for k in colours:
            for d in ds:
                arrive(sum(k.side[h, d], []))
        return [(h, k, f, d) for k in colours for d in ds for f in (k.fl, k.fr)]

    def opposite_hop(h):
        for k in colours:
            k.opposite[h] = sum((group(h, k, k.fo, z, at_z(zat(way))) for way in (1, -1)), [])

    def opposite_done(h):
        for k in colours:
            arrive(k.opposite[h])
        return [(h, k, k.fo, d) for k in colours for d in (-1, 1)]

    def far_way(k):
        return 1 - 2 * k.c

    def gather_rows(h):
        phase(f"g_r{h}")
        for k in colours:
            arrive(k.start[h])
            if h == 1:
                hop(h, k, 1, 1)
                hop(h, k, -1, 1)
            spread(h, k, 0)

    def z_round(h, n):
        phase(f"g_z{n}h{h}")
        for k in colours:
            for way in (1, -1):
                if n < 4 or way == far_way(k):
                    arrive(k.hops[h, way, n])
                    if n < 3 or (n == 3 and way == far_way(k)):
                        hop(h, k, way, n + 1)
            for d in (-n, n) if n < 4 else (4,):
                spread(h, k, d)

    for k in colours:
        k.hops, k.side, k.start, k.last, k.opposite = {}, {}, {}, {}, {}
    z_send(0)
    phase("dist1a")
    c_p.wait_recv()
    distances(1, 0, 4)
    z_send(1)
    phase("dist1b")
    distances(1, 4, 2)
    early = list(used)
    z_sum(0)
    phase("dist1c")
    distances(1, 6, 2)
    eye = lane_eye(LANES)
    for b in range(ROWS // LANES):
        part = pv[pl.ds(b * LANES, LANES), :].astype(jnp.float32)
        square = to_row(jnp.sum(part * part, axis=1, keepdims=True), eye)
        lanes = pl.ds(b * LANES, LANES)
        cost_ref[:, lanes] = (square + jnp.min(best[:, lanes], axis=0, keepdims=True)) * (1.0 / 1024)
    z_sum(1)
    for copy in early:
        copy.wait_send()
    gather_rows(0)
    z_round(0, 1)
    gather_rows(1)
    across(0, 0)
    phase("g_f0")
    finish(own_done(0, 0, -1, 1) + first_done(0, 0))
    z_round(0, 2)
    z_round(1, 1)
    across(1, 0)
    phase("g_f1")
    done = last_done(0, 0)
    opposite_hop(0)
    finish(own_done(0, -2, 2) + own_done(1, 0) + done)
    z_round(0, 3)
    z_round(1, 2)
    across(0, -2, 2)
    phase("g_f2")
    done = last_done(1, 0)
    opposite_hop(1)
    finish(own_done(0, -3, 3) + own_done(1, -1, 1) + first_done(0, -2, 2) + first_done(1, 0) + sides_done(0, -1, 1) + done)
    z_round(0, 4)
    z_round(1, 3)
    across(0, -3, 3)
    across(1, -2, 2)
    phase("g_f3")
    finish(own_done(0, 4) + own_done(1, -2, 2) + opposite_done(0))
    z_round(1, 4)
    across(0, 4)
    across(1, *(d for d in (-3, 3) if (1, d) not in STRAIGHT))
    phase("g_f4")
    finish(own_done(1, -3, 3, 4) + first_done(0, -3, 3) + first_done(1, -2, 2) + last_done(0, -2, 2) + sides_done(1, -1, 1))
    across(1, *(d for d in (4,) if (1, d) not in STRAIGHT))
    phase("g_f5")
    finish(first_done(0, 4) + first_done(1, *(d for d in (-3, 3, 4) if (1, d) not in STRAIGHT)) + last_done(0, -3, 3) + opposite_done(1))
    phase("g_f6")
    finish(last_done(0, 4) + last_done(1, -2, 2))
    phase("g_f7")
    finish(last_done(1, -3, 3))
    phase("g_f8")
    finish(last_done(1, 4))
    phase("w_send")
    for copy in used[len(early) :]:
        copy.wait_send()
    phase(None)
    assert len(used) == N_COPIES, len(used)


N_COPIES = 382
STRAIGHT = ((1, 4),)


def put_kernel(rows_ref, cost_ref, rows_hbm, cost_hbm, sems):
    puts = [pltpu.make_async_copy(cost_ref, cost_hbm, sems.at[N])]
    for q in range(N):
        rows = pl.ds(q * CROWS, CROWS)
        puts.append(pltpu.make_async_copy(rows_ref.at[rows], rows_hbm.at[rows], sems.at[q]))
    for put in puts:
        put.start()
    for put in puts:
        put.wait()


def shards(points, centroids, assign, keep_mask):
    vmem = pl.BlockSpec(memory_space=pltpu.VMEM)
    hbm = pl.BlockSpec(memory_space=pltpu.HBM)
    dma = pltpu.SemaphoreType.DMA
    f32, i32, bf16 = jnp.float32, jnp.int32, jnp.bfloat16
    args = (points, centroids, assign.reshape(1, ROWS), keep_mask.reshape(1, ROWS))
    rows, cost = pl.pallas_call(
        update_kernel,
        out_shape=(
            jax.ShapeDtypeStruct((2048, 1024), f32),
            jax.ShapeDtypeStruct((1, ROWS), f32),
        ),
        in_specs=[hbm] * 4,
        out_specs=(vmem, vmem),
        scratch_shapes=[
            pltpu.VMEM((2, 2, N, N, NZ, PAIRS, LANES), i32),
            pltpu.VMEM((2, 2, N, N, NZ, 1, LANES), f32),
            pltpu.VMEM((ROWS, 1024), bf16),
            pltpu.VMEM((2, 2048, 1024), bf16),
            pltpu.VMEM((2, 1, ROWS), i32),
            pltpu.VMEM((2 * ROWS, 2 * LANES), bf16),
            pltpu.VMEM((2, 6 * ROWS, LANES), bf16),
            pltpu.VMEM((1, 2 * ROWS), i32),
            pltpu.VMEM((2, 1, 6 * ROWS), i32),
            pltpu.VMEM((2, 2, ROWS // 2, LANES), bf16),
            pltpu.VMEM((8, ROWS), f32),
            pltpu.VMEM((2, N, 2, HROWS, LANES), f32),
            pltpu.VMEM((2, N, 2, HROWS, LANES), bf16),
            pltpu.VMEM((2, 3, 2, NZ, PAIRS, LANES), i32),
            pltpu.VMEM((2, 3, 2, 2, 2, LANES), f32),
            pltpu.VMEM((2, 3, 2, NZ, PAIRS, LANES), i32),
            pltpu.VMEM((2, 3, 2, 2, 2, LANES), f32),
            pltpu.VMEM((2, NZ, 2, PAIRS, LANES), i32),
            pltpu.VMEM((2, 2, 4, LANES), f32),
            pltpu.VMEM((2, NZ - 1, 2, PAIRS, LANES), i32),
            pltpu.VMEM((2, NZ - 1, 4, LANES), f32),
            dma((N_COPIES,)), dma((N_COPIES,)), dma((6,)),
        ],
        compiler_params=pltpu.CompilerParams(
            collective_id=0, has_side_effects=True, vmem_limit_bytes=40 * 1024 * 1024
        ),
    )(*(pltpu.with_memory_space_constraint(a, pltpu.HBM) for a in args))
    new_centroids, cost = pl.pallas_call(
        put_kernel,
        out_shape=(jax.ShapeDtypeStruct((2048, 1024), f32), jax.ShapeDtypeStruct((1, ROWS), f32)),
        in_specs=[vmem] * 2,
        out_specs=(hbm, hbm),
        scratch_shapes=[dma((N + 1,))],
        compiler_params=pltpu.CompilerParams(vmem_limit_bytes=1024 * 1024),
        cost_estimate=pl.CostEstimate(flops=0, bytes_accessed=16 << 20, transcendentals=0),
    )(rows, cost)
    return new_centroids, cost.reshape(ROWS)


def solution(mesh):
    grid = Mesh(mesh.devices.reshape(NZ, N, N, 2), ("z", "y", "x", "mp"))
    rows = ("z", "y", "x", "mp")
    in_specs = (P(rows, None), P("mp", None), P(rows), P(rows))
    out_specs = (P("mp", None), P(rows))
    return jax.shard_map(shards, mesh=grid, in_specs=in_specs, out_specs=out_specs, check_vma=False)
```

time: 78 us -> 73.4 us (0.941); the launches traced: 76.5 us -> 72.8 us
  Pallas kernels: 75.9 us -> 72 us
    pallas_call x1, Pallas kernels: 72.5 us -> 68.7 us  [shards(): pl.pallas_call(update_kernel, out_shape=(jax.ShapeDtypeStruct((2048, 1024...]
where the time goes in v5:
time: 73.4 us; the launch traced here: 72.8 us
  Pallas kernels  72 us (98%)
  between operations  0.8 us (1%)
    pallas_call x1, Pallas kernels, shards(): pl.pallas_call(update_kernel, out_shape=(jax.ShapeDtypeStruct((2048, 1024...  68.7 us
    pallas_call x1, Pallas kernels, shards(): pl.pallas_call(put_kernel, out_shape=(jax.ShapeDtypeStruct((2048, 1024),...  3.38 us

profile of v5, /device:TPU:2, one launch (start us, length us, event | category | flops | bytes accessed | tf_op | source)
XLA Modules:
  0.0 72.8 jit_solution(5434785347354726372)
XLA Ops:
  0.6 68.7 %shard_map.59 = (f32[2048,1024]{1,0:T(8,128)S(1)}, f32[1,512]{1,0:T(1,128)S(1)}) custom-call(bf16[512,1024]{1,0:T(8,128)(2,1)} %p_hbm.1, bf16[2048,1024]{1,0:T(8,128)(2,1)} %c_hbm.1, s32[1,512]{1,0:T(1,128)} %bitcast.3, s32[1,512]{1,0:T(1,128)} %bitcast.4), custom_call_target="tpu_custom_call" | custom-call | tf_op jit(solution)/shard_map/pallas_call | solution.py:557
  69.3 3.4 %shard_map.60 = (f32[2048,1024]{1,0:T(8,128)}, f32[1,512]{1,0:T(1,128)}) custom-call(f32[2048,1024]{1,0:T(8,128)S(1)} %get-tuple-element.6.rows_ref, f32[1,512]{1,0:T(1,128)S(1)} %get-tuple-element.7.cost_ref), custom_call_target="tpu_custom_call" | custom-call | bytes 16777216 | tf_op jit(solution)/shard_map/pallas_call | solution.py:593

commit v6 on v5

--- a/solution.py
+++ b/solution.py
@@ -253,15 +253,14 @@
     for k in colours:
         arrive(k.from_o)
         k.three = to_partner(k, 6, 7)
+    phase("acc2")
+    accumulate_others(colours[1], 2, 2)
     phase("w_plr")
     for k in colours:
         arrive(k.two)
-    phase("acc2")
-    accumulate_others(colours[1], 2, 4)
     phase("w_po")
     for k in colours:
         arrive(k.three)
-    colours[0].rest, colours[1].rest = (4, 4), (6, 2)
 
     def pack(c, q, h, words, aux):
         for b in range(HROWS // LANES):
@@ -289,7 +288,7 @@
     for k in colours:
         k.sums = {}
     for k, s, q in order:
-        accumulate(k.c, *k.rest, q)
+        accumulate(k.c, 4, 4, q)
         send_sums(k, s, q, 0)
     phase("y_packq")
     for k, s, q in order:
@@ -380,12 +379,15 @@
         targets = (k.fr, k.fl, k.fo) if (h, d) in STRAIGHT else (k.fr, k.fl)
         k.side[h, d] = [group(h, k, k.f, zat(d), k.at_f(to)) for to in targets]
 
+    def relayed(h, ds):
+        return [d for d in ds if (h, d) not in STRAIGHT]
+
     def left_first(d):
         return d in (0, 1, 2, 3)
 
     def across(h, *ds):
         phase(f"g_x{h}")
-        for d in ds:
+        for d in relayed(h, ds):
             for k in colours:
                 from_left, from_right = k.side[h, d]
                 if left_first(d):
@@ -412,7 +414,7 @@
         return [(h, k, k.f, d) for k in colours for d in ds]
 
     def first_done(h, *ds):
-        return [(h, k, k.fl if left_first(d) else k.fr, d) for k in colours for d in ds]
+        return [(h, k, k.fl if left_first(d) else k.fr, d) for k in colours for d in relayed(h, ds)]
 
     def last_done(h, *ds):
         groups = []
@@ -514,27 +516,29 @@
     finish(own_done(0, 4) + own_done(1, -2, 2) + opposite_done(0))
     z_round(1, 4)
     across(0, 4)
-    across(1, *(d for d in (-3, 3) if (1, d) not in STRAIGHT))
+    across(1, -3, 3)
     phase("g_f4")
     finish(own_done(1, -3, 3, 4) + first_done(0, -3, 3) + first_done(1, -2, 2) + last_done(0, -2, 2) + sides_done(1, -1, 1))
-    across(1, *(d for d in (4,) if (1, d) not in STRAIGHT))
+    across(1, 4)
     phase("g_f5")
-    finish(first_done(0, 4) + first_done(1, *(d for d in (-3, 3, 4) if (1, d) not in STRAIGHT)) + last_done(0, -3, 3) + opposite_done(1))
+    finish(first_done(0, 4) + first_done(1, -3, 3, 4) + last_done(0, -3, 3) + opposite_done(1))
     phase("g_f6")
     finish(last_done(0, 4) + last_done(1, -2, 2))
     phase("g_f7")
     finish(last_done(1, -3, 3))
+    for copy in used[len(early) : -24]:
+        copy.wait_send()
     phase("g_f8")
     finish(last_done(1, 4))
     phase("w_send")
-    for copy in used[len(early) :]:
+    for copy in used[-24:]:
         copy.wait_send()
     phase(None)
     assert len(used) == N_COPIES, len(used)
 
 
 N_COPIES = 382
-STRAIGHT = ((1, 4),)
+STRAIGHT = ((1, 4), (1, 3), (1, -3), (0, 4))
 
 
 def put_kernel(rows_ref, cost_ref, rows_hbm, cost_hbm, sems):

time: 73.4 us -> 73.5 us (level)
  no operation moved by 1% of the time
where the time goes in v6:
time: 73.5 us; the launch traced here: 73.4 us
  Pallas kernels  72.6 us (99%)
  between operations  0.8 us (1%)
    pallas_call x1, Pallas kernels, shards(): pl.pallas_call(update_kernel, out_shape=(jax.ShapeDtypeStruct((2048, 1024...  69.2 us
    pallas_call x1, Pallas kernels, shards(): pl.pallas_call(put_kernel, out_shape=(jax.ShapeDtypeStruct((2048, 1024),...  3.38 us

profile of v6, /device:TPU:2, one launch (start us, length us, event | category | flops | bytes accessed | tf_op | source)
XLA Modules:
  0.0 73.4 jit_solution(14100227727832127366)
XLA Ops:
  0.6 69.2 %shard_map.59 = (f32[2048,1024]{1,0:T(8,128)S(1)}, f32[1,512]{1,0:T(1,128)S(1)}) custom-call(bf16[512,1024]{1,0:T(8,128)(2,1)} %p_hbm.1, bf16[2048,1024]{1,0:T(8,128)(2,1)} %c_hbm.1, s32[1,512]{1,0:T(1,128)} %bitcast.3, s32[1,512]{1,0:T(1,128)} %bitcast.4), custom_call_target="tpu_custom_call" | custom-call | tf_op jit(solution)/shard_map/pallas_call | solution.py:561
  69.8 3.4 %shard_map.60 = (f32[2048,1024]{1,0:T(8,128)}, f32[1,512]{1,0:T(1,128)}) custom-call(f32[2048,1024]{1,0:T(8,128)S(1)} %get-tuple-element.6.rows_ref, f32[1,512]{1,0:T(1,128)S(1)} %get-tuple-element.7.cost_ref), custom_call_target="tpu_custom_call" | custom-call | bytes 16777216 | tf_op jit(solution)/shard_map/pallas_call | solution.py:597

commit v7 on v6

--- a/solution.py
+++ b/solution.py
@@ -538,7 +538,7 @@
 
 
 N_COPIES = 382
-STRAIGHT = ((1, 4), (1, 3), (1, -3), (0, 4))
+STRAIGHT = ((1, 4), (1, 3), (1, -3), (0, 4), (0, 3), (0, -3))
 
 
 def put_kernel(rows_ref, cost_ref, rows_hbm, cost_hbm, sems):

time: 73.5 us -> 73.5 us (level)
  no operation moved by 1% of the time
where the time goes in v7:
time: 73.5 us; the launch traced here: 73.3 us
  Pallas kernels  72.5 us (99%)
  between operations  0.8 us (1%)
    pallas_call x1, Pallas kernels, shards(): pl.pallas_call(update_kernel, out_shape=(jax.ShapeDtypeStruct((2048, 1024...  69.1 us
    pallas_call x1, Pallas kernels, shards(): pl.pallas_call(put_kernel, out_shape=(jax.ShapeDtypeStruct((2048, 1024),...  3.38 us

profile of v7, /device:TPU:2, one launch (start us, length us, event | category | flops | bytes accessed | tf_op | source)
XLA Modules:
  0.0 73.3 jit_solution(300391013752056873)
XLA Ops:
  0.6 69.1 %shard_map.59 = (f32[2048,1024]{1,0:T(8,128)S(1)}, f32[1,512]{1,0:T(1,128)S(1)}) custom-call(bf16[512,1024]{1,0:T(8,128)(2,1)} %p_hbm.1, bf16[2048,1024]{1,0:T(8,128)(2,1)} %c_hbm.1, s32[1,512]{1,0:T(1,128)} %bitcast.3, s32[1,512]{1,0:T(1,128)} %bitcast.4), custom_call_target="tpu_custom_call" | custom-call | tf_op jit(solution)/shard_map/pallas_call | solution.py:561
  69.7 3.4 %shard_map.60 = (f32[2048,1024]{1,0:T(8,128)}, f32[1,512]{1,0:T(1,128)}) custom-call(f32[2048,1024]{1,0:T(8,128)S(1)} %get-tuple-element.6.rows_ref, f32[1,512]{1,0:T(1,128)S(1)} %get-tuple-element.7.cost_ref), custom_call_target="tpu_custom_call" | custom-call | bytes 16777216 | tf_op jit(solution)/shard_map/pallas_call | solution.py:597
